TPU v7x, 32 devices: a 4x4x1 block of a 4x4x8 slice. The times are simulated.
32 devices in a mesh: dp: 1 (over z), row: 4 (over y), col: 8 (over x, core).
Axes of the slice: x: 4, y: 4, z: 1, core: 2. Of those that a mesh axis runs over, the one named last changes fastest.
The devices are a block of a 4x4x8 slice.
Arguments:
- x: bfloat16 [32768, 256], P(('dp', 'row', 'col'))
- route_idx: int32 [32768, 8], P(('dp', 'row', 'col'))
- gates: float32 [32768, 8], P(('dp', 'row', 'col'))
- w1: bfloat16 [64, 256, 128], P(('row', 'col'))
- w3: bfloat16 [64, 256, 128], P(('row', 'col'))
- w2: bfloat16 [64, 128, 256], P(('row', 'col'))
- dy: bfloat16 [32768, 256], P(('dp', 'row', 'col'))
Outputs:
- output 1: bfloat16 [32768, 256], P(('dp', 'row', 'col'))
- output 2: bfloat16 [32768, 256], P(('dp', 'row', 'col'))
- output 3: float32 [32768, 8], P(('dp', 'row', 'col'))
- output 4: float32 [64, 256, 128], P(('dp', 'row', 'col'))
- output 5: float32 [64, 256, 128], P(('dp', 'row', 'col'))
- output 6: float32 [64, 128, 256], P(('dp', 'row', 'col'))
All inputs are finite; a program needn't handle non-finite values.
Results may differ from a plain program's by a relative error of at most 0.001.
Values are sent between devices in bfloat16 or wider.
A program may use at most 768 MiB of HBM per device.

v0:
```python
import jax
import jax.numpy as jnp
from jax import lax
from jax.sharding import PartitionSpec as P


def slot_positions(ridx, ne, cap):
    tok, top = ridx.shape
    n = tok * top
    ef = ridx.reshape(n)
    order = jnp.argsort(ef, stable=True).astype(jnp.int32)
    es = ef[order]
    first = jnp.searchsorted(es, es, side='left').astype(jnp.int32)
    rank = jnp.arange(n, dtype=jnp.int32) - first
    pos = jnp.zeros((n,), jnp.int32).at[order].set(es * cap + rank)
    inv = jnp.full((ne * cap,), n, jnp.int32).at[pos].set(jnp.arange(n, dtype=jnp.int32))
    return pos, inv


def to_experts(buf, nd, el, cap):
    d = buf.shape[-1]
    return buf.reshape(nd, el, cap, d).transpose(1, 0, 2, 3).reshape(el, nd * cap, d)


def from_experts(buf, nd, el, cap):
    d = buf.shape[-1]
    return buf.reshape(el, nd, cap, d).transpose(1, 0, 2, 3).reshape(nd, el * cap, d)


def expert_forward(xe, w1, w3, w2):
    u = jnp.einsum('ecd,edf->ecf', xe, w1, preferred_element_type=jnp.float32).astype(jnp.bfloat16)
    v = jnp.einsum('ecd,edf->ecf', xe, w3, preferred_element_type=jnp.float32).astype(jnp.bfloat16)
    uf = u.astype(jnp.float32)
    a = (uf * jax.nn.sigmoid(uf) * v.astype(jnp.float32)).astype(jnp.bfloat16)
    o = jnp.einsum('ecf,efd->ecd', a, w2, preferred_element_type=jnp.float32).astype(jnp.bfloat16)
    return u, v, a, o


def expert_backward(xe, u, v, a, doe, w1, w3, w2):
    gw2 = jnp.einsum('ecf,ecd->efd', a, doe, preferred_element_type=jnp.float32)
    da = jnp.einsum('ecd,efd->ecf', doe, w2, preferred_element_type=jnp.float32)
    uf = u.astype(jnp.float32)
    vf = v.astype(jnp.float32)
    sg = jax.nn.sigmoid(uf)
    du = (da * vf * sg * (1.0 + uf * (1.0 - sg))).astype(jnp.bfloat16)
    dv = (da * uf * sg).astype(jnp.bfloat16)
    gw1 = jnp.einsum('ecd,ecf->edf', xe, du, preferred_element_type=jnp.float32)
    gw3 = jnp.einsum('ecd,ecf->edf', xe, dv, preferred_element_type=jnp.float32)
    dxe = (jnp.einsum('ecf,edf->ecd', du, w1, preferred_element_type=jnp.float32) + jnp.einsum('ecf,edf->ecd', dv, w3, preferred_element_type=jnp.float32)).astype(jnp.bfloat16)
    return gw1, gw3, gw2, dxe


def solution(mesh):
    nd = mesh.shape['row'] * mesh.shape['col']
    grp = ('row', 'col')
    tspec = P(('dp', 'row', 'col'), None)
    wspec = P(grp, None, None)
    gspec = P(('dp', 'row', 'col'), None, None)

    def exchange(buf):
        return lax.all_to_all(buf, grp, 0, 0, tiled=True)

    def local(x, ridx, gates, w1, w3, w2, dy):
        tok, d = x.shape
        top = ridx.shape[1]
        el = w1.shape[0]
        ne = el * nd
        cap = (4 * tok * top + ne - 1) // ne
        n = tok * top
        pos, inv = slot_positions(ridx, ne, cap)
        zrow = jnp.zeros((1, d), x.dtype)
        send = jnp.concatenate([x, zrow])[inv // top].reshape(nd, el * cap, d)
        xe = to_experts(exchange(send), nd, el, cap)
        u, v, a, oe = expert_forward(xe, w1, w3, w2)
        ret = exchange(from_experts(oe, nd, el, cap)).reshape(ne * cap, d)
        ob = ret[pos].reshape(tok, top, d)
        y = jnp.sum(gates[:, :, None] * ob.astype(jnp.float32), axis=1).astype(jnp.bfloat16)
        dgates = jnp.einsum('td,tjd->tj', dy, ob, preferred_element_type=jnp.float32)
        do = (gates[:, :, None] * dy[:, None, :].astype(jnp.float32)).astype(jnp.bfloat16).reshape(n, d)
        dsend = jnp.concatenate([do, zrow])[inv].reshape(nd, el * cap, d)
        doe = to_experts(exchange(dsend), nd, el, cap)
        gw1, gw3, gw2, dxe = expert_backward(xe, u, v, a, doe, w1, w3, w2)
        dret = exchange(from_experts(dxe, nd, el, cap)).reshape(ne * cap, d)
        dx = jnp.sum(dret[pos].reshape(tok, top, d).astype(jnp.float32), axis=1).astype(jnp.bfloat16)
        return y, dx, dgates, gw1, gw3, gw2

    return jax.shard_map(local, mesh=mesh, in_specs=(tspec, tspec, tspec, wspec, wspec, wspec, tspec), out_specs=(tspec, tspec, tspec, gspec, gspec, gspec), check_vma=False)
```

profile of v0, /device:TPU:97, one launch (start us, length us, event | category | flops | bytes accessed | tf_op | source)
XLA Modules:
  0.0 1908.6 jit_solution(3944945167834690456)
XLA Ops:
  3.1 6.8 sort.17
  9.9 45.5 %gather_fusion.1 = s32[8192]{0:T(1024)S(1)} fusion(s32[8192]{0:T(1024)S(1)} %reshape.63, s32[8192]{0:T(1024)S(1)} %get-tuple-element.108), kind=kCustom, calls=%fused_computation.1 | custom fusion | bytes 98304 | tf_op jit(solution)/shard_map/gather | solution.py:12
  55.5 639.0 %while.25 = (s32[]{:T(128)}, u32[8192]{0:T(1024)S(1)}, u32[8192]{0:T(1024)S(1)}, s32[8192]{0:T(1024)S(1)}, s32[]{:T(128)}, /*index=5*/s32[]{:T(128)}, s32[]{}) while((s32[]{:T(128)}, u32[8192]{0:T(1024)S(1)}, u32[8192]{0:T(1024)S(1)}, s32[8192]{0:T(1024)S(1)}, s32[]{:T(128)}, /*index=5*/s32[]{:T(128)}, s32[]{}) %tuple.45), condition=%wide.region_2.3_spmd.clone, body=%wide.region_1.2_spmd.clone.sunk | while | flops 155652 | bytes 540773 | solution.py:13
  55.5 45.5 %gather_fusion = s32[8192]{0:T(1024)S(1)} fusion(s32[8192]{0:T(1024)S(1)} %get-tuple-element.156, u32[8192]{0:T(1024)S(1)} %broadcast_clamp_fusion.4), kind=kCustom, calls=%fused_computation.clone.clone.1 | custom fusion | bytes 98304 | tf_op jit(solution)/shard_map/jit(searchsorted)/jit(_searchsorted_scan_impl)/vmap(jit(_searchsorted_scan_impl))/while/body/eval_jaxpr/gather | solution.py:13
  101.2 45.5 %gather_fusion = s32[8192]{0:T(1024)S(1)} fusion(s32[8192]{0:T(1024)S(1)} %get-tuple-element.156, u32[8192]{0:T(1024)S(1)} %broadcast_clamp_fusion.4), kind=kCustom, calls=%fused_computation.clone.clone.1 | custom fusion | bytes 98304 | tf_op jit(solution)/shard_map/jit(searchsorted)/jit(_searchsorted_scan_impl)/vmap(jit(_searchsorted_scan_impl))/while/body/eval_jaxpr/gather | solution.py:13
  146.8 45.5 %gather_fusion = s32[8192]{0:T(1024)S(1)} fusion(s32[8192]{0:T(1024)S(1)} %get-tuple-element.156, u32[8192]{0:T(1024)S(1)} %broadcast_clamp_fusion.4), kind=kCustom, calls=%fused_computation.clone.clone.1 | custom fusion | bytes 98304 | tf_op jit(solution)/shard_map/jit(searchsorted)/jit(_searchsorted_scan_impl)/vmap(jit(_searchsorted_scan_impl))/while/body/eval_jaxpr/gather | solution.py:13
  192.5 45.5 %gather_fusion = s32[8192]{0:T(1024)S(1)} fusion(s32[8192]{0:T(1024)S(1)} %get-tuple-element.156, u32[8192]{0:T(1024)S(1)} %broadcast_clamp_fusion.4), kind=kCustom, calls=%fused_computation.clone.clone.1 | custom fusion | bytes 98304 | tf_op jit(solution)/shard_map/jit(searchsorted)/jit(_searchsorted_scan_impl)/vmap(jit(_searchsorted_scan_impl))/while/body/eval_jaxpr/gather | solution.py:13
  238.1 45.5 %gather_fusion = s32[8192]{0:T(1024)S(1)} fusion(s32[8192]{0:T(1024)S(1)} %get-tuple-element.156, u32[8192]{0:T(1024)S(1)} %broadcast_clamp_fusion.4), kind=kCustom, calls=%fused_computation.clone.clone.1 | custom fusion | bytes 98304 | tf_op jit(solution)/shard_map/jit(searchsorted)/jit(_searchsorted_scan_impl)/vmap(jit(_searchsorted_scan_impl))/while/body/eval_jaxpr/gather | solution.py:13
  283.7 45.5 %gather_fusion = s32[8192]{0:T(1024)S(1)} fusion(s32[8192]{0:T(1024)S(1)} %get-tuple-element.156, u32[8192]{0:T(1024)S(1)} %broadcast_clamp_fusion.4), kind=kCustom, calls=%fused_computation.clone.clone.1 | custom fusion | bytes 98304 | tf_op jit(solution)/shard_map/jit(searchsorted)/jit(_searchsorted_scan_impl)/vmap(jit(_searchsorted_scan_impl))/while/body/eval_jaxpr/gather | solution.py:13
  329.4 45.5 %gather_fusion = s32[8192]{0:T(1024)S(1)} fusion(s32[8192]{0:T(1024)S(1)} %get-tuple-element.156, u32[8192]{0:T(1024)S(1)} %broadcast_clamp_fusion.4), kind=kCustom, calls=%fused_computation.clone.clone.1 | custom fusion | bytes 98304 | tf_op jit(solution)/shard_map/jit(searchsorted)/jit(_searchsorted_scan_impl)/vmap(jit(_searchsorted_scan_impl))/while/body/eval_jaxpr/gather | solution.py:13
  375.0 45.5 %gather_fusion = s32[8192]{0:T(1024)S(1)} fusion(s32[8192]{0:T(1024)S(1)} %get-tuple-element.156, u32[8192]{0:T(1024)S(1)} %broadcast_clamp_fusion.4), kind=kCustom, calls=%fused_computation.clone.clone.1 | custom fusion | bytes 98304 | tf_op jit(solution)/shard_map/jit(searchsorted)/jit(_searchsorted_scan_impl)/vmap(jit(_searchsorted_scan_impl))/while/body/eval_jaxpr/gather | solution.py:13
  420.7 45.5 %gather_fusion = s32[8192]{0:T(1024)S(1)} fusion(s32[8192]{0:T(1024)S(1)} %get-tuple-element.156, u32[8192]{0:T(1024)S(1)} %broadcast_clamp_fusion.4), kind=kCustom, calls=%fused_computation.clone.clone.1 | custom fusion | bytes 98304 | tf_op jit(solution)/shard_map/jit(searchsorted)/jit(_searchsorted_scan_impl)/vmap(jit(_searchsorted_scan_impl))/while/body/eval_jaxpr/gather | solution.py:13
  466.3 45.5 %gather_fusion = s32[8192]{0:T(1024)S(1)} fusion(s32[8192]{0:T(1024)S(1)} %get-tuple-element.156, u32[8192]{0:T(1024)S(1)} %broadcast_clamp_fusion.4), kind=kCustom, calls=%fused_computation.clone.clone.1 | custom fusion | bytes 98304 | tf_op jit(solution)/shard_map/jit(searchsorted)/jit(_searchsorted_scan_impl)/vmap(jit(_searchsorted_scan_impl))/while/body/eval_jaxpr/gather | solution.py:13
  511.9 45.5 %gather_fusion = s32[8192]{0:T(1024)S(1)} fusion(s32[8192]{0:T(1024)S(1)} %get-tuple-element.156, u32[8192]{0:T(1024)S(1)} %broadcast_clamp_fusion.4), kind=kCustom, calls=%fused_computation.clone.clone.1 | custom fusion | bytes 98304 | tf_op jit(solution)/shard_map/jit(searchsorted)/jit(_searchsorted_scan_impl)/vmap(jit(_searchsorted_scan_impl))/while/body/eval_jaxpr/gather | solution.py:13
  557.6 45.5 %gather_fusion = s32[8192]{0:T(1024)S(1)} fusion(s32[8192]{0:T(1024)S(1)} %get-tuple-element.156, u32[8192]{0:T(1024)S(1)} %broadcast_clamp_fusion.4), kind=kCustom, calls=%fused_computation.clone.clone.1 | custom fusion | bytes 98304 | tf_op jit(solution)/shard_map/jit(searchsorted)/jit(_searchsorted_scan_impl)/vmap(jit(_searchsorted_scan_impl))/while/body/eval_jaxpr/gather | solution.py:13
  603.2 45.5 %gather_fusion = s32[8192]{0:T(1024)S(1)} fusion(s32[8192]{0:T(1024)S(1)} %get-tuple-element.156, u32[8192]{0:T(1024)S(1)} %broadcast_clamp_fusion.4), kind=kCustom, calls=%fused_computation.clone.clone.1 | custom fusion | bytes 98304 | tf_op jit(solution)/shard_map/jit(searchsorted)/jit(_searchsorted_scan_impl)/vmap(jit(_searchsorted_scan_impl))/while/body/eval_jaxpr/gather | solution.py:13
  648.9 45.5 %gather_fusion = s32[8192]{0:T(1024)S(1)} fusion(s32[8192]{0:T(1024)S(1)} %get-tuple-element.156, u32[8192]{0:T(1024)S(1)} %broadcast_clamp_fusion.4), kind=kCustom, calls=%fused_computation.clone.clone.1 | custom fusion | bytes 98304 | tf_op jit(solution)/shard_map/jit(searchsorted)/jit(_searchsorted_scan_impl)/vmap(jit(_searchsorted_scan_impl))/while/body/eval_jaxpr/gather | solution.py:13
  694.5 30.5 %scatter_custom_fusion = s32[8192]{0:T(1024)S(1)} fusion(s32[8192]{0:T(1024)S(1)} %get-tuple-element.109, s32[8192]{0:T(1024)S(1)} %subtract_add_fusion, s32[]{:T(128)} %constant.56.clone.1), kind=kCustom, calls=%fused_computation.57 | custom fusion | bytes 32772 | tf_op jit(solution)/shard_map/scatter | solution.py:15
  725.6 30.5 %scatter_custom_fusion.1 = s32[32768]{0:T(1024)S(1)} fusion(s32[8192]{0:T(1024)S(1)} %get-tuple-element.107, s32[8192]{0:T(1024)S(1)} %iota.12, s32[]{:T(128)} %constant.55.clone.1), kind=kCustom, calls=%fused_computation.52 | custom fusion | bytes 131076 | tf_op jit(solution)/shard_map/scatter | solution.py:16
  756.4 5.5 fusion.10
  764.0 123.4 %gather_fusion.4 = bf16[32768,256]{1,0:T(8,128)(2,1)} fusion(bf16[8193,256]{1,0:T(8,128)(2,1)} %concatenate.7, s32[32768]{0:T(1024)S(1)} %get-tuple-element.104), kind=kCustom, calls=%fused_computation.4 | custom fusion | bytes 33685504 | tf_op jit(solution)/shard_map/gather | solution.py:80
  887.4 9.1 all-to-all-start.2
  896.6 128.7 %gather_fusion.2 = bf16[32768,256]{1,0:T(8,128)(2,1)} fusion(bf16[1025,256]{1,0:T(8,128)(2,1)S(1)} %concatenate.6, s32[32768]{0:T(1024)S(1)} %get-tuple-element.105), kind=kCustom, calls=%fused_computation.2 | custom fusion | bytes 33685504 | tf_op jit(solution)/shard_map/gather | solution.py:72
  1025.2 74.6 %all-to-all-done.2 = bf16[32,1024,256]{2,1,0:T(8,128)(2,1)} async-done(((bf16[32,1024,256]{2,1,0:T(8,128)(2,1)}), bf16[32,1024,256]{2,1,0:T(8,128)(2,1)}, u32[]{:S(2)}, u32[]{:S(2)}) %all-to-all-start.2) | async-done | bytes 16777248 | tf_op jit(solution)/shard_map/all_to_all | solution.py:61
  1099.9 37.2 %all-to-all-start = ((bf16[32,1024,256]{2,1,0:T(8,128)(2,1)}), bf16[32,1024,256]{2,1,0:T(8,128)(2,1)}, u32[]{:S(2)}, u32[]{:S(2)}) async-start(bf16[32,1024,256]{2,1,0:T(8,128)(2,1)} %bitcast.62), calls=%async_computation | async-start | bytes 33554432 | tf_op jit(solution)/shard_map/all_to_all | solution.py:61
  1137.0 13.7 copy.22
  1150.8 191.7 %all-to-all-done = bf16[32,1024,256]{2,1,0:T(8,128)(2,1)} async-done(((bf16[32,1024,256]{2,1,0:T(8,128)(2,1)}), bf16[32,1024,256]{2,1,0:T(8,128)(2,1)}, u32[]{:S(2)}, u32[]{:S(2)}) %all-to-all-start) | async-done | bytes 16777248 | tf_op jit(solution)/shard_map/all_to_all | solution.py:61
  1342.5 8.1 copy.19
  1350.7 7.3 convolution_convert_fusion.1
  1358.9 6.7 convolution_convert_fusion.2
  1365.6 22.3 %fusion.9 = (bf16[2,16384,128]{2,1,0:T(8,128)(2,1)}, bf16[2,16384,128]{2,1,0:T(8,128)(2,1)}, bf16[2,16384,128]{2,1,0:T(8,128)(2,1)S(1)}) fusion(bf16[2,16384,128]{2,1,0:T(8,128)(2,1)} %convolution_convert_fusion.2, bf16[2,16384,128]{2,1,0:T(8,128)(2,1)} %convolution_convert_fusion.1, bf16[2,16384,256]{2,1,0:T(8,128)(2,1)} %bitcast.58, ...), kind=kOutput, calls=%fused_computation.31 | convolution fusion | flops 2222981120 | bytes 58851328 | tf_op jit(solution)/shard_map/ecd,efd->ecf/dot_general | solution.py:41
  1387.9 8.3 convolution_convert_fusion
  1396.2 13.8 copy.20
  1409.9 21.6 %all-to-all-start.1 = ((bf16[32,1024,256]{2,1,0:T(8,128)(2,1)}), bf16[32,1024,256]{2,1,0:T(8,128)(2,1)}, u32[]{:S(2)}, u32[]{:S(2)}) async-start(bf16[32,1024,256]{2,1,0:T(8,128)(2,1)} %bitcast.61), calls=%async_computation.1 | async-start | bytes 33554432 | tf_op jit(solution)/shard_map/all_to_all | solution.py:61
  1431.5 19.0 fusion.22
  1450.5 21.1 %add_convert_fusion = bf16[2,16384,256]{2,1,0:T(8,128)(2,1)} fusion(f32[2,16384,256]{2,1,0:T(8,128)} %fusion.22, bf16[2,16384,128]{2,1,0:T(8,128)(2,1)} %get-tuple-element.101, bf16[2,256,128]{2,1,0:T(8,128)(2,1)S(1)} %copy-done.9), kind=kOutput, calls=%fused_computation.12 | convolution fusion | flops 2164260864 | bytes 58851328 | tf_op jit(solution)/shard_map/ecf,edf->ecd/dot_general | solution.py:49
  1471.6 13.7 copy.23
  1485.3 139.0 %all-to-all-done.1 = bf16[32,1024,256]{2,1,0:T(8,128)(2,1)} async-done(((bf16[32,1024,256]{2,1,0:T(8,128)(2,1)}), bf16[32,1024,256]{2,1,0:T(8,128)(2,1)}, u32[]{:S(2)}, u32[]{:S(2)}) %all-to-all-start.1) | async-done | bytes 16777248 | tf_op jit(solution)/shard_map/all_to_all | solution.py:61
  1624.4 35.5 %all-to-all-start.3 = ((bf16[32,1024,256]{2,1,0:T(8,128)(2,1)}), bf16[32,1024,256]{2,1,0:T(8,128)(2,1)}, u32[]{:S(2)}, u32[]{:S(2)}) async-start(bf16[32,1024,256]{2,1,0:T(8,128)(2,1)} %bitcast.60), calls=%async_computation.3 | async-start | bytes 33554432 | tf_op jit(solution)/shard_map/all_to_all | solution.py:61
  1659.8 12.5 fusion.25
  1672.3 11.5 fusion.24
  1683.8 11.4 fusion.23
  1695.2 39.1 %gather_fusion.3 = bf16[8192,256]{1,0:T(8,128)(2,1)} fusion(bf16[32768,256]{1,0:T(8,128)(2,1)} %bitcast.7, s32[8192]{0:T(1024)S(1)} %copy-done.10), kind=kCustom, calls=%fused_computation.3 | custom fusion | bytes 8421376 | tf_op jit(solution)/shard_map/gather | solution.py:76
  1734.3 3.4 fusion.11
  1738.6 8.0 multiply_reduce_fusion
  1746.6 117.2 %all-to-all-done.3 = bf16[32,1024,256]{2,1,0:T(8,128)(2,1)} async-done(((bf16[32,1024,256]{2,1,0:T(8,128)(2,1)}), bf16[32,1024,256]{2,1,0:T(8,128)(2,1)}, u32[]{:S(2)}, u32[]{:S(2)}) %all-to-all-start.3) | async-done | bytes 16777248 | tf_op jit(solution)/shard_map/all_to_all | solution.py:61
  1863.8 38.8 %gather_fusion.5 = bf16[8192,256]{1,0:T(8,128)(2,1)} fusion(bf16[32768,256]{1,0:T(8,128)(2,1)} %bitcast.17, s32[8192]{0:T(1024)S(1)} %copy-done.10), kind=kCustom, calls=%fused_computation.5 | custom fusion | bytes 8421376 | tf_op jit(solution)/shard_map/gather | solution.py:84
  1902.6 5.8 bitcast_reduce_fusion
  (94 shorter events, 8.0 us)
Async XLA Ops:
  0.6 1364.9 %copy-start = (bf16[2,128,256]{2,1,0:T(8,128)(2,1)S(1)}, bf16[2,128,256]{2,1,0:T(8,128)(2,1)}, u32[]{:S(2)}) copy-start(bf16[2,128,256]{2,1,0:T(8,128)(2,1)} %param.14) | copy-start | bytes 393220
  1.7 53.8 %copy-start.3 = (f32[1024,8]{1,0:T(8,128)}, f32[1024,8]{1,0:T(8,128)S(1)}, u32[]{:S(2)}) copy-start(f32[1024,8]{1,0:T(8,128)S(1)} %copy.17) | copy-start | bytes 98308
  55.5 700.8 %copy-start.6 = (bf16[1024,256]{1,0:T(8,128)(2,1)S(1)}, bf16[1024,256]{1,0:T(8,128)(2,1)}, u32[]{:S(2)}) copy-start(bf16[1024,256]{1,0:T(8,128)(2,1)} %param.15) | copy-start | bytes 1572868
  887.4 9.2 copy-start.8
  887.4 212.5 %all-to-all-start.2 = ((bf16[32,1024,256]{2,1,0:T(8,128)(2,1)}), bf16[32,1024,256]{2,1,0:T(8,128)(2,1)}, u32[]{:S(2)}, u32[]{:S(2)}) async-start(bf16[32,1024,256]{2,1,0:T(8,128)(2,1)} %bitcast.63), calls=%async_computation.2 | async-start | bytes 33554432 | tf_op jit(solution)/shard_map/all_to_all | solution.py:61
  1099.9 242.7 %all-to-all-start = ((bf16[32,1024,256]{2,1,0:T(8,128)(2,1)}), bf16[32,1024,256]{2,1,0:T(8,128)(2,1)}, u32[]{:S(2)}, u32[]{:S(2)}) async-start(bf16[32,1024,256]{2,1,0:T(8,128)(2,1)} %bitcast.62), calls=%async_computation | async-start | bytes 33554432 | tf_op jit(solution)/shard_map/all_to_all | solution.py:61
  1342.5 8.1 copy-start.9
  1350.6 8.2 copy-start.1
  1350.7 8.2 copy-start.5
  1387.9 8.3 copy-start.2
  1409.9 214.5 %all-to-all-start.1 = ((bf16[32,1024,256]{2,1,0:T(8,128)(2,1)}), bf16[32,1024,256]{2,1,0:T(8,128)(2,1)}, u32[]{:S(2)}, u32[]{:S(2)}) async-start(bf16[32,1024,256]{2,1,0:T(8,128)(2,1)} %bitcast.61), calls=%async_computation.1 | async-start | bytes 33554432 | tf_op jit(solution)/shard_map/all_to_all | solution.py:61
  1624.4 239.4 %all-to-all-start.3 = ((bf16[32,1024,256]{2,1,0:T(8,128)(2,1)}), bf16[32,1024,256]{2,1,0:T(8,128)(2,1)}, u32[]{:S(2)}, u32[]{:S(2)}) async-start(bf16[32,1024,256]{2,1,0:T(8,128)(2,1)} %bitcast.60), calls=%async_computation.3 | async-start | bytes 33554432 | tf_op jit(solution)/shard_map/all_to_all | solution.py:61
  1683.8 11.4 copy-start.10
  1695.2 39.1 %copy-start.7 = (bf16[1024,256]{1,0:T(8,128)(2,1)S(1)}, bf16[1024,256]{1,0:T(8,128)(2,1)}, u32[]{:S(2)}) copy-start(bf16[1024,256]{1,0:T(8,128)(2,1)} %param.15) | copy-start | bytes 1572868
  1695.2 43.4 %copy-start.4 = (f32[1024,8]{1,0:T(8,128)S(1)}, f32[1024,8]{1,0:T(8,128)}, u32[]{:S(2)}) copy-start(f32[1024,8]{1,0:T(8,128)} %copy-done.3) | copy-start | bytes 98308
where the time goes:
time: 1940 us; the launch traced here: 1910 us
  local copies, waits for them, and re-layouts  1130 us (58%)
  waiting for transfers between devices  523 us (27%)
  matrix products  124 us (6%)
  starting transfers between devices  103 us (5%)
  other arithmetic  27.6 us (1%)
    gather x14, local copies, waits for them, and re-layouts, slot_positions(): first = jnp.searchsorted(es, es, side='left').astype(jnp.int32)  637 us
    all_to_all x4, waiting for transfers between devices, exchange(): return lax.all_to_all(buf, grp, 0, 0, tiled=True)  523 us
    gather x1, local copies, waits for them, and re-layouts, local(): send = jnp.concatenate([x, zrow])[inv // top].reshape(nd, el * cap, d)  129 us
    gather x1, local copies, waits for them, and re-layouts, local(): dsend = jnp.concatenate([do, zrow])[inv].reshape(nd, el * cap, d)  123 us
    all_to_all x4, starting transfers between devices, exchange(): return lax.all_to_all(buf, grp, 0, 0, tiled=True)  103 us
    gather x1, local copies, waits for them, and re-layouts, slot_positions(): es = ef[order]  45.5 us
    gather x1, local copies, waits for them, and re-layouts, local(): ob = ret[pos].reshape(tok, top, d)  39.1 us
    gather x1, local copies, waits for them, and re-layouts, local(): dret[pos].reshape(tok, top, d).astype(jnp.float32)  38.8 us
  transfers between devices with their start and end apart: 4, of which 4 were waited for; matrix products, arithmetic and copies ran while one was open for 15% of the time, Pallas kernels for 0%

commit v1 on v0

v1 whole, which is shorter than its diff:
```python
import functools

import jax
import jax.numpy as jnp
from jax import lax
from jax.experimental import pallas as pl
from jax.experimental.pallas import tpu as pltpu
from jax.sharding import PartitionSpec as P

RINGS = 4
SLOTS = 6
LAG = 2
MESH = pl.DeviceIdType.MESH
F32 = jnp.float32
BF16 = jnp.bfloat16


def dot(a, b):
    return jnp.dot(a, b, preferred_element_type=F32)


def tdot(a, b):
    return lax.dot_general(a, b, (((0,), (0,)), ((), ())), preferred_element_type=F32)


def neighbours(k):
    dp = lax.axis_index('dp')
    row = lax.axis_index('row')
    col = lax.axis_index('col')
    x = col // 2
    c = col % 2
    s = (row + x) % k
    last = (s + 1) // k
    first = 1 - (s + k - 1) // k
    b = 1 - c

    def at(r, q, core):
        return (dp, r % k, (q % k) * 2 + core)

    n1 = at(row + c * last, x + c * (1 - last), b)
    p1 = at(row + k - b * first, x + k - b * (1 - first), b)
    n2 = at(row + c * (1 - last), x + c * last, b)
    p2 = at(row + k - b * (1 - first), x + k - b * first, b)
    return (n1, p1), (n2, p2)


def pick(i, a, b):
    return tuple((1 - i) * p + i * q for p, q in zip(a, b))


def kernel(n, k, x_hbm, dy_hbm, g_hbm, w1_ref, w3_ref, w2_ref, w2t_ref, w13t_ref,
           y_ref, dx_ref, dg_ref, gw1_ref, gw3_ref, gw2_ref,
           xs, gs, acc, own, part, gw13, load_sem, xsend, xrecv, gsend, grecv,
           asend, arecv, xfree, afree):
    t = xs.shape[2] // 2
    d = x_hbm.shape[1]
    el, ff, _ = w2_ref.shape
    top = g_hbm.shape[0] // 2
    h1, h2 = neighbours(k)
    first_expert = (lax.axis_index('row') * lax.axis_size('col') + lax.axis_index('col')) * el

    loads = []
    for r in range(RINGS):
        rows = pl.ds(r * t, t)
        loads.append(pltpu.make_async_copy(x_hbm.at[rows], xs.at[r, 0, pl.ds(0, t)], load_sem.at[r, 0]))
        loads.append(pltpu.make_async_copy(dy_hbm.at[rows], xs.at[r, 0, pl.ds(t, t)], load_sem.at[r, 1]))
        loads.append(pltpu.make_async_copy(g_hbm.at[:, rows], gs.at[r, 0], load_sem.at[r, 2]))
    for cp in loads:
        cp.start()

    barrier = pltpu.get_barrier_semaphore()
    for dev in (*h1, *h2):
        pl.semaphore_signal(barrier, inc=1, device_id=dev, device_id_type=MESH)

    gw13[...] = jnp.zeros_like(gw13)
    gw2_ref[...] = jnp.zeros_like(gw2_ref)
    for cp in loads:
        cp.wait()
    pl.semaphore_wait(barrier, 4)

    def tile(r, slot):
        x = xs[r, slot, 0:t, :]
        dy = xs[r, slot, t:2 * t, :]
        gates = gs[r, slot, 0:top, :]
        ids = gs[r, slot, top:2 * top, :]
        hit = [ids == (first_expert + e).astype(F32) for e in range(el)]
        sub = lax.broadcasted_iota(jnp.int32, gates.shape, 0)
        rows = jnp.zeros_like(gates)
        for e in range(el):
            ge = jnp.sum(jnp.where(hit[e], gates, 0.0), axis=0, keepdims=True)
            me = jnp.max(jnp.where(hit[e], 1.0, 0.0), axis=0, keepdims=True)
            rows = jnp.where(sub == e, ge, jnp.where(sub == el + e, me, rows))
        colm = rows.T
        dyf = dy.astype(F32)
        ua = dot(x, w1_ref[...])
        va = dot(x, w3_ref[...])
        y = None
        dx = None
        dgc = jnp.zeros((t, 128), F32)
        lane = lax.broadcasted_iota(jnp.int32, dgc.shape, 1)
        dudv = []
        for e in range(el):
            g = colm[:, e:e + 1]
            m = colm[:, el + e:el + e + 1] > 0.5
            u = jnp.where(m, ua[:, e * ff:(e + 1) * ff].astype(BF16).astype(F32), 0.0)
            v = jnp.where(m, va[:, e * ff:(e + 1) * ff].astype(BF16).astype(F32), 0.0)
            s = jax.nn.sigmoid(u)
            us = u * s
            a = (us * v).astype(BF16)
            o = dot(a, w2_ref[e]).astype(BF16).astype(F32)
            yo = g * o
            y = yo if y is None else y + yo
            dgc = jnp.where(lane == e, jnp.sum(dyf * o, axis=1, keepdims=True), dgc)
            do = (g * dyf).astype(BF16)
            gw2_ref[e] += tdot(a, do)
            da = dot(do, w2t_ref[e])
            du = (da * v * s * (1.0 + u * (1.0 - s))).astype(BF16)
            dv = (da * us).astype(BF16)
            dd = jnp.concatenate([du, dv], axis=1)
            dudv.append(dd)
            de = dot(dd, w13t_ref[e]).astype(BF16).astype(F32)
            dx = de if dx is None else dx + de
        gw13[...] += tdot(x, jnp.concatenate(dudv, axis=1))
        part[0:t, :] = y
        part[t:2 * t, :] = dx
        dgr = dgc.T
        dg = jnp.zeros_like(gates)
        for e in range(el):
            dg = jnp.where(hit[e], dgr[e:e + 1, :], dg)
        part[2 * t:2 * t + top, :] = dg

    def step(i, carry):
        st = i // RINGS
        r = i % RINGS
        cyc = r // 2
        back = r % 2
        fwd = pick(cyc, h1[0], h2[0])
        bwd = pick(cyc, h1[1], h2[1])
        nxt = pick(back, fwd, bwd)
        prv = pick(back, bwd, fwd)
        slot = st % SLOTS
        into = (st + 1) % SLOTS

        def xcopy(a, b):
            return pltpu.make_async_remote_copy(
                src_ref=xs.at[r, a], dst_ref=xs.at[r, b], send_sem=xsend.at[r, a], recv_sem=xrecv.at[r, b],
                device_id=nxt, device_id_type=MESH)

        def gcopy(a, b):
            return pltpu.make_async_remote_copy(
                src_ref=gs.at[r, a], dst_ref=gs.at[r, b], send_sem=gsend.at[r, a], recv_sem=grecv.at[r, b],
                device_id=nxt, device_id_type=MESH)

        def acopy(a, b):
            return pltpu.make_async_remote_copy(
                src_ref=acc.at[r, a], dst_ref=acc.at[r, b], send_sem=asend.at[r, a], recv_sem=arecv.at[r, b],
                device_id=nxt, device_id_type=MESH)

        done = st - LAG
        dslot = (st + SLOTS - LAG) % SLOTS

        @pl.when((done >= 0) & (done <= n - 2))
        def _():
            xcopy(dslot, dslot).wait_send()
            gcopy(dslot, dslot).wait_send()

        @pl.when((done >= 0) & (done <= n - 1 - SLOTS))
        def _():
            pl.semaphore_signal(xfree.at[r], inc=1, device_id=prv, device_id_type=MESH)

        @pl.when((done >= 1) & (done <= n - 1))
        def _():
            acopy(dslot, dslot).wait_send()

        @pl.when((done >= 1) & (done <= n - SLOTS))
        def _():
            pl.semaphore_signal(afree.at[r], inc=1, device_id=prv, device_id_type=MESH)

        @pl.when(st <= n - 1)
        def _():
            @pl.when(st >= 1)
            def _():
                gcopy(slot, slot).wait_recv()
                xcopy(slot, slot).wait_recv()

            @pl.when(st <= n - 2)
            def _():
                @pl.when(st + 1 >= SLOTS)
                def _():
                    pl.semaphore_wait(xfree.at[r], 1)

                gcopy(slot, into).start()
                xcopy(slot, into).start()

            tile(r, slot)

            @pl.when(st == 0)
            def _():
                own[r] = part[...]

            @pl.when(st == 1)
            def _():
                acc[r, slot] = part[...]

            @pl.when(st >= 2)
            def _():
                acopy(slot, slot).wait_recv()
                acc[r, slot] += part[...]

            @pl.when(st >= 1)
            def _():
                @pl.when(st >= SLOTS)
                def _():
                    pl.semaphore_wait(afree.at[r], 1)

                acopy(slot, into).start()

        @pl.when(st == n)
        def _():
            acopy(slot, slot).wait_recv()
            total = acc[r, slot] + own[r]
            rows = pl.ds(pl.multiple_of(r * t, t), t)
            y_ref[rows, :] = total[0:t].astype(BF16)
            dx_ref[rows, :] = total[t:2 * t].astype(BF16)
            dg_ref[r] = total[2 * t:2 * t + top]

        return carry

    lax.fori_loop(0, (n + 2) * RINGS, step, 0)

    for e in range(el):
        gw1_ref[e] = gw13[:, 2 * e * ff:(2 * e + 1) * ff]
        gw3_ref[e] = gw13[:, (2 * e + 1) * ff:(2 * e + 2) * ff]


def solution(mesh):
    k = mesh.shape['row']
    n = k * mesh.shape['col']
    grp = ('row', 'col')
    tspec = P(('dp', 'row', 'col'), None)
    wspec = P(grp, None, None)
    gspec = P(('dp', 'row', 'col'), None, None)

    def local(x, ridx, gates, w1, w3, w2, dy):
        tok, d = x.shape
        top = ridx.shape[1]
        el, ff, _ = w2.shape
        t = tok // RINGS
        g = jnp.concatenate([gates.T, ridx.T.astype(F32)], axis=0)
        w1c = jnp.concatenate([w1[e] for e in range(el)], axis=1)
        w3c = jnp.concatenate([w3[e] for e in range(el)], axis=1)
        w2t = w2.transpose(0, 2, 1)
        w13t = jnp.concatenate([w1.transpose(0, 2, 1), w3.transpose(0, 2, 1)], axis=1)
        rows = 2 * t + top
        vmem = pl.BlockSpec(memory_space=pltpu.VMEM)
        hbm = pl.BlockSpec(memory_space=pl.ANY)
        dma = pltpu.SemaphoreType.DMA((RINGS, SLOTS))
        flops = 2 * n * tok * el * 9 * d * ff
        y, dx, dg, gw1, gw3, gw2 = pl.pallas_call(
            functools.partial(kernel, n, k),
            out_shape=(
                jax.ShapeDtypeStruct((tok, d), BF16),
                jax.ShapeDtypeStruct((tok, d), BF16),
                jax.ShapeDtypeStruct((RINGS, top, t), F32),
                jax.ShapeDtypeStruct((el, d, ff), F32),
                jax.ShapeDtypeStruct((el, d, ff), F32),
                jax.ShapeDtypeStruct((el, ff, d), F32),
            ),
            in_specs=[hbm, hbm, hbm] + [vmem] * 5,
            out_specs=tuple([vmem] * 6),
            scratch_shapes=[
                pltpu.VMEM((RINGS, SLOTS, 2 * t, d), BF16),
                pltpu.VMEM((RINGS, SLOTS, 2 * top, t), F32),
                pltpu.VMEM((RINGS, SLOTS, rows, d), F32),
                pltpu.VMEM((RINGS, rows, d), F32),
                pltpu.VMEM((rows, d), F32),
                pltpu.VMEM((d, 2 * el * ff), F32),
                pltpu.SemaphoreType.DMA((RINGS, 3)),
                dma, dma, dma, dma, dma, dma,
                pltpu.SemaphoreType.REGULAR((RINGS,)),
                pltpu.SemaphoreType.REGULAR((RINGS,)),
            ],
            compiler_params=pltpu.CompilerParams(
                collective_id=0, has_side_effects=True, vmem_limit_bytes=56 * 1024 * 1024),
            cost_estimate=pl.CostEstimate(flops=flops, bytes_accessed=4 * tok * d * 2, transcendentals=n * tok * el * ff),
            name='moe_ring',
        )(x, dy, g, w1c, w3c, w2, w2t, w13t)
        return y, dx, dg.transpose(0, 2, 1).reshape(tok, top), gw1, gw3, gw2

    return jax.shard_map(local, mesh=mesh, in_specs=(tspec, tspec, tspec, wspec, wspec, wspec, tspec), out_specs=(tspec, tspec, tspec, gspec, gspec, gspec), check_vma=False)
```

time: 1940 us -> 318 us (0.16); the launches traced: 1910 us -> 314 us
  local copies, waits for them, and re-layouts: 1130 us -> 8.15 us
  waiting for transfers between devices: 523 us -> 0 us
  Pallas kernels: 0 us -> 301 us
  matrix products: 124 us -> 0 us
  starting transfers between devices: 103 us -> 0 us
  other arithmetic: 27.6 us -> 3.64 us
    gather x19 -> x0, local copies, waits for them, and re-layouts: 1010 us -> none  [the longest x14 637 us: slot_positions(): first = jnp.searchsorted(es, es, side='left').astype(jnp.int32)]
    all_to_all x4 -> x0, waiting for transfers between devices: 523 us -> none  [exchange(): return lax.all_to_all(buf, grp, 0, 0, tiled=True)]
    pallas_call x0 -> x1, Pallas kernels: none -> 301 us  [local(): pl.pallas_call(functools.partial(kernel, n, k), out_shape=(jax.ShapeDtype...]
    dot_general x10 -> x0, matrix products: 124 us -> none  [the longest x1 22.3 us: expert_backward(): da = jnp.einsum('ecd,efd->ecf', doe, w2, preferred_element_type=jnp.float32)]
    all_to_all x4 -> x0, starting transfers between devices: 103 us -> none  [exchange(): return lax.all_to_all(buf, grp, 0, 0, tiled=True)]
    scatter x2 -> x0, local copies, waits for them, and re-layouts: 61 us -> none  [the longest x1 30.5 us: slot_positions(): jnp.full((ne * cap,), n, jnp.int32).at[pos]]
    reshape x3 -> x0, local copies, waits for them, and re-layouts: 27.7 us -> none  [the longest x2 27.5 us: from_experts(): buf.reshape(el, nd, cap, d).transpose(1, 0, 2, 3).reshape(nd, el * cap, d)]
    transpose x2 -> x0, local copies, waits for them, and re-layouts: 21.9 us -> none  [to_experts(): buf.reshape(nd, el, cap, d).transpose(1, 0, 2, 3).reshape(el, nd * cap, d)]
  transfers between devices with their start and end apart: 4 -> 0, of which waited for: 4 -> 0; matrix products, arithmetic and copies ran while one was open for 15% -> 0% of each run, Pallas kernels for 0% -> 0%
where the time goes in v1:
time: 318 us; the launch traced here: 314 us
  Pallas kernels  301 us (95%)
  local copies, waits for them, and re-layouts  8.15 us (3%)
  other arithmetic  3.64 us (1%)
    pallas_call x1, Pallas kernels, local(): pl.pallas_call(functools.partial(kernel, n, k), out_shape=(jax.ShapeDtype...  301 us
    unnamed x25, local copies, waits for them, and re-layouts  8.13 us

profile of v1, /device:TPU:97, one launch (start us, length us, event | category | flops | bytes accessed | tf_op | source)
XLA Modules:
  0.0 313.8 jit_solution(13988140072774838524)
XLA Ops:
  0.6 0.0 copy-start.1
  0.6 0.8 convert_bitcast_fusion
  1.4 1.4 pad_maximum_fusion.3.g_hbm
  2.8 0.0 copy-done.1
  2.8 0.0 copy-start.2
  2.8 0.1 copy.14
  3.0 0.8 copy-done.2
  3.7 0.1 copy.15
  3.9 0.0 copy-start.6
  3.9 0.7 pad_maximum_fusion.w13t_ref
  4.6 0.2 copy-done.6
  4.8 0.8 copy.13
  5.6 0.7 pad_maximum_fusion.1
  6.3 301.3 %moe_ring.1 = (bf16[1024,256]{1,0:T(8,128)(2,1)}, bf16[1024,256]{1,0:T(8,128)(2,1)}, f32[4,8,256]{2,1,0:T(8,128)}, f32[2,256,128]{2,1,0:T(8,128)}, f32[2,256,128]{2,1,0:T(8,128)}, /*index=5*/f32[2,128,256]{2,1,0:T(8,128)}) custom-call(bf16[1024,256]{1,0:T(8,128)(2,1)} %x_hbm.1, bf16[1024,256]{1,0:T(8,128)(2,1)} %dy_hbm.1, ...), custom_call_target="tpu_custom_call" | custom-call | flops 38654705664 | bytes 2097152 | tf_op jit(solution)/shard_map/moe_ring/pallas_call | solution.py:259
  307.7 0.0 copy-start
  307.7 1.9 copy.22
  309.6 0.0 copy-done
  309.6 0.0 copy-start.7
  309.6 0.0 copy-start.5
  309.6 0.8 copy.23
  310.4 0.0 copy-done.7
  310.4 0.6 copy.24
  311.0 0.0 copy-done.5
  311.0 0.0 copy-start.4
  311.0 0.7 copy.25
  311.8 0.3 copy-done.4
  312.1 0.0 copy-start.3
  312.1 0.7 copy.26
  312.8 0.3 copy-done.3
  313.1 0.7 copy.27
  (2 shorter events, 0.0 us)
Async XLA Ops:
  0.6 2.2 copy-start.1
  2.8 0.9 copy-start.2
  3.9 1.0 copy-start.6
  307.7 1.9 copy-start
  309.6 0.8 copy-start.7
  309.6 1.4 copy-start.5
  311.0 1.0 copy-start.4
  312.1 1.0 copy-start.3

commit v2 on v1

--- a/solution.py
+++ b/solution.py
@@ -57,6 +57,7 @@
     el, ff, _ = w2_ref.shape
     top = g_hbm.shape[0] // 2
     h1, h2 = neighbours(k)
+    core = lax.axis_index('col') % 2
     first_expert = (lax.axis_index('row') * lax.axis_size('col') + lax.axis_index('col')) * el
 
     loads = []
@@ -130,16 +131,18 @@
         part[2 * t:2 * t + top, :] = dg
 
     def step(i, carry):
-        st = i // RINGS
-        r = i % RINGS
-        cyc = r // 2
-        back = r % 2
+        link = (i % RINGS) // 2
+        st = i // RINGS - 1 + link
+        cyc = i % 2
+        back = core + link * (1 - 2 * core)
+        r = 2 * cyc + back
         fwd = pick(cyc, h1[0], h2[0])
         bwd = pick(cyc, h1[1], h2[1])
         nxt = pick(back, fwd, bwd)
         prv = pick(back, bwd, fwd)
-        slot = st % SLOTS
+        slot = (st + SLOTS) % SLOTS
         into = (st + 1) % SLOTS
+        xslot = slot + (SLOTS - slot) * ((1 - link) * ((st + 1) // n))
 
         def xcopy(a, b):
             return pltpu.make_async_remote_copy(
@@ -156,15 +159,35 @@
                 src_ref=acc.at[r, a], dst_ref=acc.at[r, b], send_sem=asend.at[r, a], recv_sem=arecv.at[r, b],
                 device_id=nxt, device_id_type=MESH)
 
+        def xlast():
+            return pltpu.make_async_remote_copy(
+                src_ref=xs.at[r, 0], dst_ref=xs.at[r, SLOTS], send_sem=xsend.at[r, SLOTS], recv_sem=xrecv.at[r, SLOTS],
+                device_id=prv, device_id_type=MESH)
+
+        def glast():
+            return pltpu.make_async_remote_copy(
+                src_ref=gs.at[r, 0], dst_ref=gs.at[r, SLOTS], send_sem=gsend.at[r, SLOTS], recv_sem=grecv.at[r, SLOTS],
+                device_id=prv, device_id_type=MESH)
+
+        def afirst():
+            return pltpu.make_async_remote_copy(
+                src_ref=acc.at[r, 1], dst_ref=acc.at[r, SLOTS], send_sem=asend.at[r, 1], recv_sem=arecv.at[r, SLOTS],
+                device_id=prv, device_id_type=MESH)
+
         done = st - LAG
-        dslot = (st + SLOTS - LAG) % SLOTS
-
-        @pl.when((done >= 0) & (done <= n - 2))
+        dslot = (st + 2 * SLOTS - LAG) % SLOTS
+
+        @pl.when((done >= 0) & (done <= n - 2 - link))
         def _():
             xcopy(dslot, dslot).wait_send()
             gcopy(dslot, dslot).wait_send()
 
-        @pl.when((done >= 0) & (done <= n - 1 - SLOTS))
+        @pl.when((done == 0) & (link == 1))
+        def _():
+            xlast().wait_send()
+            glast().wait_send()
+
+        @pl.when((done >= 0) & (done <= n - 2 - SLOTS + link))
         def _():
             pl.semaphore_signal(xfree.at[r], inc=1, device_id=prv, device_id_type=MESH)
 
@@ -176,14 +199,14 @@
         def _():
             pl.semaphore_signal(afree.at[r], inc=1, device_id=prv, device_id_type=MESH)
 
-        @pl.when(st <= n - 1)
+        @pl.when((st >= 0) & (st <= n - 1))
         def _():
             @pl.when(st >= 1)
             def _():
-                gcopy(slot, slot).wait_recv()
-                xcopy(slot, slot).wait_recv()
-
-            @pl.when(st <= n - 2)
+                gcopy(xslot, xslot).wait_recv()
+                xcopy(xslot, xslot).wait_recv()
+
+            @pl.when(st <= n - 2 - link)
             def _():
                 @pl.when(st + 1 >= SLOTS)
                 def _():
@@ -192,22 +215,31 @@
                 gcopy(slot, into).start()
                 xcopy(slot, into).start()
 
-            tile(r, slot)
+            @pl.when((st == 0) & (link == 1))
+            def _():
+                glast().start()
+                xlast().start()
+
+            tile(r, xslot)
 
             @pl.when(st == 0)
             def _():
                 own[r] = part[...]
 
-            @pl.when(st == 1)
+            @pl.when((st >= 1) & (st <= 2 - link))
             def _():
                 acc[r, slot] = part[...]
 
-            @pl.when(st >= 2)
+            @pl.when(st >= 3 - link)
             def _():
                 acopy(slot, slot).wait_recv()
                 acc[r, slot] += part[...]
 
-            @pl.when(st >= 1)
+            @pl.when((st == 1) & (link == 1))
+            def _():
+                afirst().start()
+
+            @pl.when(st >= 1 + link)
             def _():
                 @pl.when(st >= SLOTS)
                 def _():
@@ -218,7 +250,14 @@
         @pl.when(st == n)
         def _():
             acopy(slot, slot).wait_recv()
-            total = acc[r, slot] + own[r]
+            own[r] += acc[r, slot]
+
+            @pl.when(link == 0)
+            def _():
+                acopy(SLOTS, SLOTS).wait_recv()
+                own[r] += acc[r, SLOTS]
+
+            total = own[r]
             rows = pl.ds(pl.multiple_of(r * t, t), t)
             y_ref[rows, :] = total[0:t].astype(BF16)
             dx_ref[rows, :] = total[t:2 * t].astype(BF16)
@@ -226,7 +265,7 @@
 
         return carry
 
-    lax.fori_loop(0, (n + 2) * RINGS, step, 0)
+    lax.fori_loop(0, (n + LAG + 1) * RINGS, step, 0)
 
     for e in range(el):
         gw1_ref[e] = gw13[:, 2 * e * ff:(2 * e + 1) * ff]
@@ -254,7 +293,7 @@
         rows = 2 * t + top
         vmem = pl.BlockSpec(memory_space=pltpu.VMEM)
         hbm = pl.BlockSpec(memory_space=pl.ANY)
-        dma = pltpu.SemaphoreType.DMA((RINGS, SLOTS))
+        dma = pltpu.SemaphoreType.DMA((RINGS, SLOTS + 1))
         flops = 2 * n * tok * el * 9 * d * ff
         y, dx, dg, gw1, gw3, gw2 = pl.pallas_call(
             functools.partial(kernel, n, k),
@@ -269,9 +308,9 @@
             in_specs=[hbm, hbm, hbm] + [vmem] * 5,
             out_specs=tuple([vmem] * 6),
             scratch_shapes=[
-                pltpu.VMEM((RINGS, SLOTS, 2 * t, d), BF16),
-                pltpu.VMEM((RINGS, SLOTS, 2 * top, t), F32),
-                pltpu.VMEM((RINGS, SLOTS, rows, d), F32),
+                pltpu.VMEM((RINGS, SLOTS + 1, 2 * t, d), BF16),
+                pltpu.VMEM((RINGS, SLOTS + 1, 2 * top, t), F32),
+                pltpu.VMEM((RINGS, SLOTS + 1, rows, d), F32),
                 pltpu.VMEM((RINGS, rows, d), F32),
                 pltpu.VMEM((rows, d), F32),
                 pltpu.VMEM((d, 2 * el * ff), F32),

time: 318 us -> 291 us (0.915); the launches traced: 314 us -> 290 us
  Pallas kernels: 301 us -> 278 us
    pallas_call x1, Pallas kernels: 301 us -> 278 us  [local(): pl.pallas_call(functools.partial(kernel, n, k), out_shape=(jax.ShapeDtype...]
where the time goes in v2:
time: 291 us; the launch traced here: 290 us
  Pallas kernels  278 us (96%)
  local copies, waits for them, and re-layouts  8.15 us (3%)
  other arithmetic  3.64 us (1%)
    pallas_call x1, Pallas kernels, local(): pl.pallas_call(functools.partial(kernel, n, k), out_shape=(jax.ShapeDtype...  278 us
    unnamed x25, local copies, waits for them, and re-layouts  8.13 us

profile of v2, /device:TPU:97, one launch (start us, length us, event | category | flops | bytes accessed | tf_op | source)
XLA Modules:
  0.0 290.3 jit_solution(319679002596700987)
XLA Ops:
  0.6 0.0 copy-start.1
  0.6 0.8 convert_bitcast_fusion
  1.4 1.4 pad_maximum_fusion.3.g_hbm
  2.8 0.0 copy-done.1
  2.8 0.0 copy-start.2
  2.8 0.1 copy.14
  3.0 0.8 copy-done.2
  3.7 0.1 copy.15
  3.9 0.0 copy-start.6
  3.9 0.7 pad_maximum_fusion.w13t_ref
  4.6 0.2 copy-done.6
  4.8 0.8 copy.13
  5.6 0.7 pad_maximum_fusion.1
  6.3 277.9 %moe_ring.1 = (bf16[1024,256]{1,0:T(8,128)(2,1)}, bf16[1024,256]{1,0:T(8,128)(2,1)}, f32[4,8,256]{2,1,0:T(8,128)}, f32[2,256,128]{2,1,0:T(8,128)}, f32[2,256,128]{2,1,0:T(8,128)}, /*index=5*/f32[2,128,256]{2,1,0:T(8,128)}) custom-call(bf16[1024,256]{1,0:T(8,128)(2,1)} %x_hbm.1, bf16[1024,256]{1,0:T(8,128)(2,1)} %dy_hbm.1, ...), custom_call_target="tpu_custom_call" | custom-call | flops 38654705664 | bytes 2097152 | tf_op jit(solution)/shard_map/moe_ring/pallas_call | solution.py:298
  284.2 0.0 copy-start
  284.2 1.9 copy.22
  286.1 0.0 copy-done
  286.1 0.0 copy-start.7
  286.1 0.0 copy-start.5
  286.1 0.8 copy.23
  286.9 0.0 copy-done.7
  286.9 0.6 copy.24
  287.5 0.0 copy-done.5
  287.6 0.0 copy-start.4
  287.6 0.7 copy.25
  288.3 0.3 copy-done.4
  288.6 0.0 copy-start.3
  288.6 0.7 copy.26
  289.3 0.3 copy-done.3
  289.6 0.7 copy.27
  (2 shorter events, 0.0 us)
Async XLA Ops:
  0.6 2.2 copy-start.1
  2.8 0.9 copy-start.2
  3.9 1.0 copy-start.6
  284.2 1.9 copy-start
  286.1 0.8 copy-start.7
  286.1 1.4 copy-start.5
  287.6 1.0 copy-start.4
  288.6 1.0 copy-start.3

commit v3 on v1

v3 whole, which is shorter than its diff:
```python
import functools

import jax
import jax.numpy as jnp
from jax import lax
from jax.experimental import pallas as pl
from jax.experimental.pallas import tpu as pltpu
from jax.sharding import PartitionSpec as P

RINGS = 4
SLOTS = 6
LAG = 2
MESH = pl.DeviceIdType.MESH
F32 = jnp.float32
BF16 = jnp.bfloat16


def dot(a, b):
    return jnp.dot(a, b, preferred_element_type=F32)


def tdot(a, b):
    return lax.dot_general(a, b, (((0,), (0,)), ((), ())), preferred_element_type=F32)


def neighbours(k):
    dp = lax.axis_index('dp')
    row = lax.axis_index('row')
    col = lax.axis_index('col')
    x = col // 2
    c = col % 2
    s = (row + x) % k
    last = (s + 1) // k
    first = 1 - (s + k - 1) // k
    b = 1 - c

    def at(r, q, core):
        return (dp, r % k, (q % k) * 2 + core)

    n1 = at(row + c * last, x + c * (1 - last), b)
    p1 = at(row + k - b * first, x + k - b * (1 - first), b)
    n2 = at(row + c * (1 - last), x + c * last, b)
    p2 = at(row + k - b * (1 - first), x + k - b * first, b)
    return (n1, p1), (n2, p2)


def pick(i, a, b):
    return tuple((1 - i) * p + i * q for p, q in zip(a, b))


def kernel(n, k, x_hbm, dy_hbm, g_hbm, id_hbm, w1_hbm, w3_hbm, w2_hbm,
           y_ref, dx_ref, dg_ref, gw1_ref, gw3_ref, gw2_ref,
           xs, gs, acc, own, part, gw13, ids, w1_ref, w3_ref, w2_ref, w2t_ref, w13t_ref,
           load_sem, xsend, xrecv, gsend, grecv, asend, arecv, xfree, afree):
    t = gs.shape[3]
    d = x_hbm.shape[1]
    el, ff, _ = w2_hbm.shape
    top = g_hbm.shape[0]
    h1, h2 = neighbours(k)
    core = lax.axis_index('col') % 2
    first_expert = (lax.axis_index('row') * lax.axis_size('col') + lax.axis_index('col')) * el

    def load(src, dst, i, j):
        cp = pltpu.make_async_copy(src, dst, load_sem.at[i, j])
        cp.start()
        return cp

    first = [load(id_hbm, ids, RINGS, 0)]
    for r in range(RINGS):
        rows = pl.ds(r * t, t)
        first.append(load(x_hbm.at[rows], xs.at[r, 0, pl.ds(0, t)], r, 0))
        first.append(load(dy_hbm.at[rows], xs.at[r, 0, pl.ds(t, t)], r, 1))
        first.append(load(g_hbm.at[:, rows], gs.at[r, 0], r, 2))
    later = [load(w2_hbm, w2_ref, RINGS, 1)]
    for e in range(el):
        cols = pl.ds(e * ff, ff)
        later.append(load(w1_hbm.at[e], w1_ref.at[:, cols], RINGS + 1, e))
        later.append(load(w3_hbm.at[e], w3_ref.at[:, cols], RINGS + 2, e))

    barrier = pltpu.get_barrier_semaphore()
    for dev in (*h1, *h2):
        pl.semaphore_signal(barrier, inc=1, device_id=dev, device_id_type=MESH)

    for cp in first:
        cp.wait()
    for r in range(RINGS):
        xs[r, 0, 2 * t:2 * t + top, :] = ids[:, r * t:(r + 1) * t].astype(F32).astype(BF16)
    gw13[...] = jnp.zeros_like(gw13)
    gw2_ref[...] = jnp.zeros_like(gw2_ref)
    pl.semaphore_wait(barrier, 4)

    def tile(r, slot):
        x = xs[r, slot, 0:t, :]
        dy = xs[r, slot, t:2 * t, :]
        gates = gs[r, slot, 0:top, :]
        dest = xs[r, slot, 2 * t:2 * t + top, :].astype(F32)
        hit = [dest == (first_expert + e).astype(F32) for e in range(el)]
        sub = lax.broadcasted_iota(jnp.int32, gates.shape, 0)
        rows = jnp.zeros_like(gates)
        for e in range(el):
            ge = jnp.sum(jnp.where(hit[e], gates, 0.0), axis=0, keepdims=True)
            me = jnp.max(jnp.where(hit[e], 1.0, 0.0), axis=0, keepdims=True)
            rows = jnp.where(sub == e, ge, jnp.where(sub == el + e, me, rows))
        colm = rows.T
        dyf = dy.astype(F32)
        ua = dot(x, w1_ref[...])
        va = dot(x, w3_ref[...])
        y = None
        dx = None
        dgc = jnp.zeros((t, 128), F32)
        lane = lax.broadcasted_iota(jnp.int32, dgc.shape, 1)
        dudv = []
        for e in range(el):
            g = colm[:, e:e + 1]
            m = colm[:, el + e:el + e + 1] > 0.5
            u = jnp.where(m, ua[:, e * ff:(e + 1) * ff].astype(BF16).astype(F32), 0.0)
            v = jnp.where(m, va[:, e * ff:(e + 1) * ff].astype(BF16).astype(F32), 0.0)
            s = jax.nn.sigmoid(u)
            us = u * s
            a = (us * v).astype(BF16)
            o = dot(a, w2_ref[e]).astype(BF16).astype(F32)
            yo = g * o
            y = yo if y is None else y + yo
            dgc = jnp.where(lane == e, jnp.sum(dyf * o, axis=1, keepdims=True), dgc)
            do = (g * dyf).astype(BF16)
            gw2_ref[e] += tdot(a, do)
            da = dot(do, w2t_ref[e])
            du = (da * v * s * (1.0 + u * (1.0 - s))).astype(BF16)
            dv = (da * us).astype(BF16)
            dd = jnp.concatenate([du, dv], axis=1)
            dudv.append(dd)
            de = dot(dd, w13t_ref[e]).astype(BF16).astype(F32)
            dx = de if dx is None else dx + de
        gw13[...] += tdot(x, jnp.concatenate(dudv, axis=1))
        part[0:t, :] = y
        part[t:2 * t, :] = dx
        dgr = dgc.T
        dg = jnp.zeros_like(gates)
        for e in range(el):
            dg = jnp.where(hit[e], dgr[e:e + 1, :], dg)
        part[2 * t:2 * t + top, :] = dg

    def ring(i):
        link = i // 2
        cyc = i % 2
        back = core + link * (1 - 2 * core)
        fwd = pick(cyc, h1[0], h2[0])
        bwd = pick(cyc, h1[1], h2[1])
        return link, 2 * cyc + back, pick(back, fwd, bwd), pick(back, bwd, fwd)

    def send(buf, sends, recvs, r, a, b, dev, s=None):
        return pltpu.make_async_remote_copy(
            src_ref=buf.at[r, a], dst_ref=buf.at[r, b], send_sem=sends.at[r, a if s is None else s],
            recv_sem=recvs.at[r, b], device_id=dev, device_id_type=MESH)

    def xcopies(r, a, b, dev, s=None):
        return send(gs, gsend, grecv, r, a, b, dev, s), send(xs, xsend, xrecv, r, a, b, dev, s)

    def begin(i, carry):
        link, r, nxt, prv = ring(RINGS - 1 - i)
        for cp in xcopies(r, 0, 1, nxt):
            cp.start()

        @pl.when(link == 1)
        def _():
            for cp in xcopies(r, 0, SLOTS, prv, SLOTS):
                cp.start()

        return carry

    lax.fori_loop(0, RINGS, begin, 0)

    for cp in later:
        cp.wait()
    for e in range(el):
        cols = slice(e * ff, (e + 1) * ff)
        w2t_ref[e] = w2_ref[e].astype(F32).T.astype(BF16)
        w13t_ref[e, 0:ff, :] = w1_ref[:, cols].astype(F32).T.astype(BF16)
        w13t_ref[e, ff:2 * ff, :] = w3_ref[:, cols].astype(F32).T.astype(BF16)

    def step(i, carry):
        link, r, nxt, prv = ring(i % RINGS)
        st = i // RINGS - 1 + link
        slot = (st + SLOTS) % SLOTS
        into = (st + 1) % SLOTS
        two = (st + 2) % SLOTS
        xslot = slot + (SLOTS - slot) * ((1 - link) * ((st + 1) // n))
        into_x = into + (SLOTS - into) * ((1 - link) * ((st + 2) // n))
        gone = (st + SLOTS - 1) % SLOTS
        done = st - LAG
        dslot = (st + 2 * SLOTS - LAG) % SLOTS

        def acopy(a, b):
            return send(acc, asend, arecv, r, a, b, nxt)

        @pl.when((st >= 1) & (st <= n - 1 - link))
        def _():
            for cp in xcopies(r, gone, gone, nxt):
                cp.wait_send()

        @pl.when((st == 1) & (link == 1))
        def _():
            for cp in xcopies(r, 0, SLOTS, prv, SLOTS):
                cp.wait_send()

        @pl.when((st >= 1) & (st <= n - 1 - SLOTS + link))
        def _():
            pl.semaphore_signal(xfree.at[r], inc=1, device_id=prv, device_id_type=MESH)

        @pl.when((done >= 1) & (done <= n - 1))
        def _():
            acopy(dslot, dslot).wait_send()

        @pl.when((done >= 1) & (done <= n - SLOTS))
        def _():
            pl.semaphore_signal(afree.at[r], inc=1, device_id=prv, device_id_type=MESH)

        @pl.when((st >= 0) & (st <= n - 1))
        def _():
            tile(r, xslot)

            @pl.when(st <= n - 2)
            def _():
                for cp in xcopies(r, into_x, into_x, nxt):
                    cp.wait_recv()

            @pl.when(st <= n - 3 - link)
            def _():
                @pl.when(st + 2 >= SLOTS)
                def _():
                    pl.semaphore_wait(xfree.at[r], 1)

                for cp in xcopies(r, into, two, nxt):
                    cp.start()

            @pl.when(st == 0)
            def _():
                own[r] = part[...]

            @pl.when((st >= 1) & (st <= 2 - link))
            def _():
                acc[r, slot] = part[...]

            @pl.when(st >= 3 - link)
            def _():
                acopy(slot, slot).wait_recv()
                acc[r, slot] += part[...]

            @pl.when((st == 1) & (link == 1))
            def _():
                send(acc, asend, arecv, r, 1, SLOTS, prv).start()

            @pl.when(st >= 1 + link)
            def _():
                @pl.when(st >= SLOTS)
                def _():
                    pl.semaphore_wait(afree.at[r], 1)

                acopy(slot, into).start()

        @pl.when(i == n * RINGS + 2)
        def _():
            for e in range(el):
                gw1_ref[e] = gw13[:, 2 * e * ff:(2 * e + 1) * ff]
                gw3_ref[e] = gw13[:, (2 * e + 1) * ff:(2 * e + 2) * ff]

        @pl.when((st == n - 1) & (link == 0))
        def _():
            acopy(SLOTS, SLOTS).wait_recv()
            own[r] += acc[r, SLOTS]

        @pl.when(st == n)
        def _():
            acopy(slot, slot).wait_recv()
            total = acc[r, slot] + own[r]
            rows = pl.ds(pl.multiple_of(r * t, t), t)
            y_ref[rows, :] = total[0:t].astype(BF16)
            dx_ref[rows, :] = total[t:2 * t].astype(BF16)
            dg_ref[r] = total[2 * t:2 * t + top]

        return carry

    lax.fori_loop(0, (n + LAG + 1) * RINGS, step, 0)


def solution(mesh):
    k = mesh.shape['row']
    n = k * mesh.shape['col']
    grp = ('row', 'col')
    tspec = P(('dp', 'row', 'col'), None)
    wspec = P(grp, None, None)
    gspec = P(('dp', 'row', 'col'), None, None)

    def local(x, ridx, gates, w1, w3, w2, dy):
        tok, d = x.shape
        top = ridx.shape[1]
        el, ff, _ = w2.shape
        t = tok // RINGS
        rows = 2 * t + top
        vmem = pl.BlockSpec(memory_space=pltpu.VMEM)
        hbm = pl.BlockSpec(memory_space=pltpu.HBM)
        dma = pltpu.SemaphoreType.DMA((RINGS, SLOTS + 1))
        flops = 2 * n * tok * el * 9 * d * ff
        y, dx, dg, gw1, gw3, gw2 = pl.pallas_call(
            functools.partial(kernel, n, k),
            out_shape=(
                jax.ShapeDtypeStruct((tok, d), BF16),
                jax.ShapeDtypeStruct((tok, d), BF16),
                jax.ShapeDtypeStruct((RINGS, top, t), F32),
                jax.ShapeDtypeStruct((el, d, ff), F32),
                jax.ShapeDtypeStruct((el, d, ff), F32),
                jax.ShapeDtypeStruct((el, ff, d), F32),
            ),
            in_specs=[hbm] * 7,
            out_specs=tuple([vmem] * 6),
            scratch_shapes=[
                pltpu.VMEM((RINGS, SLOTS + 1, rows, d), BF16),
                pltpu.VMEM((RINGS, SLOTS + 1, top, t), F32),
                pltpu.VMEM((RINGS, SLOTS + 1, rows, d), F32),
                pltpu.VMEM((RINGS, rows, d), F32),
                pltpu.VMEM((rows, d), F32),
                pltpu.VMEM((d, 2 * el * ff), F32),
                pltpu.VMEM((top, tok), jnp.int32),
                pltpu.VMEM((d, el * ff), BF16),
                pltpu.VMEM((d, el * ff), BF16),
                pltpu.VMEM((el, ff, d), BF16),
                pltpu.VMEM((el, d, ff), BF16),
                pltpu.VMEM((el, 2 * ff, d), BF16),
                pltpu.SemaphoreType.DMA((RINGS + 3, max(3, el))),
                dma, dma, dma, dma, dma, dma,
                pltpu.SemaphoreType.REGULAR((RINGS,)),
                pltpu.SemaphoreType.REGULAR((RINGS,)),
            ],
            compiler_params=pltpu.CompilerParams(
                collective_id=0, has_side_effects=True, vmem_limit_bytes=56 * 1024 * 1024),
            cost_estimate=pl.CostEstimate(flops=flops, bytes_accessed=4 * tok * d * 2, transcendentals=n * tok * el * ff),
            name='moe_ring',
        )(x, dy, gates.T, ridx.T, w1, w3, w2)
        return y, dx, dg.transpose(0, 2, 1).reshape(tok, top), gw1, gw3, gw2

    return jax.shard_map(local, mesh=mesh, in_specs=(tspec, tspec, tspec, wspec, wspec, wspec, tspec), out_specs=(tspec, tspec, tspec, gspec, gspec, gspec), check_vma=False)
```

time: 318 us -> 284 us (0.89); the launches traced: 314 us -> 284 us
  Pallas kernels: 301 us -> 277 us
  other arithmetic: 3.64 us -> 0 us
    pallas_call x1, Pallas kernels: 301 us -> 277 us  [local(): pl.pallas_call(functools.partial(kernel, n, k), out_shape=(jax.ShapeDtype...]
    unnamed x25 -> x16, local copies, waits for them, and re-layouts: 8.13 us -> 6.13 us
where the time goes in v3:
time: 284 us
  Pallas kernels  277 us (98%)
  local copies, waits for them, and re-layouts  6.13 us (2%)
    pallas_call x1, Pallas kernels, local(): pl.pallas_call(functools.partial(kernel, n, k), out_shape=(jax.ShapeDtype...  277 us
    unnamed x16, local copies, waits for them, and re-layouts  6.13 us

profile of v3, /device:TPU:97, one launch (start us, length us, event | category | flops | bytes accessed | tf_op | source)
XLA Modules:
  0.0 283.8 jit_solution(14998149746254753796)
XLA Ops:
  0.6 277.0 %moe_ring.1 = (bf16[1024,256]{1,0:T(8,128)(2,1)}, bf16[1024,256]{1,0:T(8,128)(2,1)}, f32[4,8,256]{2,1,0:T(8,128)}, f32[2,256,128]{2,1,0:T(8,128)}, f32[2,256,128]{2,1,0:T(8,128)}, /*index=5*/f32[2,128,256]{2,1,0:T(8,128)}) custom-call(bf16[1024,256]{1,0:T(8,128)(2,1)} %x_hbm.1, bf16[1024,256]{1,0:T(8,128)(2,1)} %dy_hbm.1, f32[8,1024]{1,0:T(8,128)} %bitcast.6, ...), custom_call_target="tpu_custom_call" | custom-call | flops 38654705664 | bytes 2097152 | tf_op jit(solution)/shard_map/moe_ring/pallas_call | solution.py:304
  277.7 0.0 copy-start
  277.7 1.9 copy.19
  279.6 0.0 copy-done
  279.6 0.0 copy-start.4
  279.6 0.0 copy-start.3
  279.6 0.8 copy.20
  280.4 0.0 copy-done.4
  280.4 0.6 copy.21
  281.0 0.0 copy-done.3
  281.0 0.0 copy-start.2
  281.0 0.7 copy.22
  281.7 0.3 copy-done.2
  282.1 0.0 copy-start.1
  282.1 0.7 copy.23
  282.8 0.3 copy-done.1
  283.1 0.7 copy.24
Async XLA Ops:
  277.7 1.9 copy-start
  279.6 0.8 copy-start.4
  279.6 1.4 copy-start.3
  281.0 1.0 copy-start.2
  282.1 1.0 copy-start.1

commit v4 on v3

--- a/solution.py
+++ b/solution.py
@@ -8,8 +8,10 @@
 from jax.sharding import PartitionSpec as P
 
 RINGS = 4
-SLOTS = 6
+SLOTS = 8
+HOME = SLOTS + 1
 LAG = 2
+OWN_STEP = 5
 MESH = pl.DeviceIdType.MESH
 F32 = jnp.float32
 BF16 = jnp.bfloat16
@@ -49,9 +51,9 @@
 
 
 def kernel(n, k, x_hbm, dy_hbm, g_hbm, id_hbm, w1_hbm, w3_hbm, w2_hbm,
-           y_ref, dx_ref, dg_ref, gw1_ref, gw3_ref, gw2_ref,
-           xs, gs, acc, own, part, gw13, ids, w1_ref, w3_ref, w2_ref, w2t_ref, w13t_ref,
-           load_sem, xsend, xrecv, gsend, grecv, asend, arecv, xfree, afree):
+           y_hbm, dx_hbm, dg_hbm, gw13_hbm, gw2_hbm,
+           xs, gs, acc, own, part, gw13, gw2_ref, out, ids, w1_ref, w3_ref, w2_ref, w2t_ref, w13t_ref,
+           load_sem, out_sem, xsend, xrecv, gsend, grecv, asend, arecv, xfree, afree):
     t = gs.shape[3]
     d = x_hbm.shape[1]
     el, ff, _ = w2_hbm.shape
@@ -68,9 +70,9 @@
     first = [load(id_hbm, ids, RINGS, 0)]
     for r in range(RINGS):
         rows = pl.ds(r * t, t)
-        first.append(load(x_hbm.at[rows], xs.at[r, 0, pl.ds(0, t)], r, 0))
-        first.append(load(dy_hbm.at[rows], xs.at[r, 0, pl.ds(t, t)], r, 1))
-        first.append(load(g_hbm.at[:, rows], gs.at[r, 0], r, 2))
+        first.append(load(x_hbm.at[rows], xs.at[r, HOME, pl.ds(0, t)], r, 0))
+        first.append(load(dy_hbm.at[rows], xs.at[r, HOME, pl.ds(t, t)], r, 1))
+        first.append(load(g_hbm.at[:, rows], gs.at[r, HOME], r, 2))
     later = [load(w2_hbm, w2_ref, RINGS, 1)]
     for e in range(el):
         cols = pl.ds(e * ff, ff)
@@ -84,7 +86,7 @@
     for cp in first:
         cp.wait()
     for r in range(RINGS):
-        xs[r, 0, 2 * t:2 * t + top, :] = ids[:, r * t:(r + 1) * t].astype(F32).astype(BF16)
+        xs[r, HOME, 2 * t:2 * t + top, :] = ids[:, r * t:(r + 1) * t].astype(F32).astype(BF16)
     gw13[...] = jnp.zeros_like(gw13)
     gw2_ref[...] = jnp.zeros_like(gw2_ref)
     pl.semaphore_wait(barrier, 4)
@@ -158,12 +160,12 @@
 
     def begin(i, carry):
         link, r, nxt, prv = ring(RINGS - 1 - i)
-        for cp in xcopies(r, 0, 1, nxt):
+        for cp in xcopies(r, HOME, 1, nxt):
             cp.start()
 
         @pl.when(link == 1)
         def _():
-            for cp in xcopies(r, 0, SLOTS, prv, SLOTS):
+            for cp in xcopies(r, HOME, SLOTS, prv, SLOTS):
                 cp.start()
 
         return carry
@@ -177,6 +179,16 @@
         w2t_ref[e] = w2_ref[e].astype(F32).T.astype(BF16)
         w13t_ref[e, 0:ff, :] = w1_ref[:, cols].astype(F32).T.astype(BF16)
         w13t_ref[e, ff:2 * ff, :] = w3_ref[:, cols].astype(F32).T.astype(BF16)
+
+    def weight_grads():
+        return (pltpu.make_async_copy(gw13, gw13_hbm, out_sem.at[RINGS, 0]),
+                pltpu.make_async_copy(gw2_ref, gw2_hbm, out_sem.at[RINGS, 1]))
+
+    def results(r):
+        rows = pl.ds(pl.multiple_of(r * t, t), t)
+        return (pltpu.make_async_copy(out.at[r, pl.ds(0, t)], y_hbm.at[rows], out_sem.at[r, 0]),
+                pltpu.make_async_copy(out.at[r, pl.ds(t, t)], dx_hbm.at[rows], out_sem.at[r, 1]),
+                pltpu.make_async_copy(own.at[r, pl.ds(2 * t, top)], dg_hbm.at[r], out_sem.at[r, 2]))
 
     def step(i, carry):
         link, r, nxt, prv = ring(i % RINGS)
@@ -193,17 +205,22 @@
         def acopy(a, b):
             return send(acc, asend, arecv, r, a, b, nxt)
 
-        @pl.when((st >= 1) & (st <= n - 1 - link))
+        @pl.when((st >= 2) & (st <= n - 1 - link))
         def _():
             for cp in xcopies(r, gone, gone, nxt):
                 cp.wait_send()
 
-        @pl.when((st == 1) & (link == 1))
-        def _():
-            for cp in xcopies(r, 0, SLOTS, prv, SLOTS):
+        @pl.when(st == 2)
+        def _():
+            for cp in xcopies(r, HOME, HOME, nxt):
                 cp.wait_send()
 
-        @pl.when((st >= 1) & (st <= n - 1 - SLOTS + link))
+        @pl.when((st == 2) & (link == 1))
+        def _():
+            for cp in xcopies(r, HOME, SLOTS, prv, SLOTS):
+                cp.wait_send()
+
+        @pl.when((st >= 2) & (st <= n - 1 - SLOTS + link))
         def _():
             pl.semaphore_signal(xfree.at[r], inc=1, device_id=prv, device_id_type=MESH)
 
@@ -217,7 +234,9 @@
 
         @pl.when((st >= 0) & (st <= n - 1))
         def _():
-            tile(r, xslot)
+            @pl.when(st >= 1)
+            def _():
+                tile(r, xslot)
 
             @pl.when(st <= n - 2)
             def _():
@@ -226,16 +245,12 @@
 
             @pl.when(st <= n - 3 - link)
             def _():
-                @pl.when(st + 2 >= SLOTS)
+                @pl.when(st + 2 > SLOTS)
                 def _():
                     pl.semaphore_wait(xfree.at[r], 1)
 
                 for cp in xcopies(r, into, two, nxt):
                     cp.start()
-
-            @pl.when(st == 0)
-            def _():
-                own[r] = part[...]
 
             @pl.when((st >= 1) & (st <= 2 - link))
             def _():
@@ -258,11 +273,15 @@
 
                 acopy(slot, into).start()
 
+        @pl.when(st == OWN_STEP)
+        def _():
+            tile(r, HOME)
+            own[r] = part[...]
+
         @pl.when(i == n * RINGS + 2)
         def _():
-            for e in range(el):
-                gw1_ref[e] = gw13[:, 2 * e * ff:(2 * e + 1) * ff]
-                gw3_ref[e] = gw13[:, (2 * e + 1) * ff:(2 * e + 2) * ff]
+            for cp in weight_grads():
+                cp.start()
 
         @pl.when((st == n - 1) & (link == 0))
         def _():
@@ -272,15 +291,53 @@
         @pl.when(st == n)
         def _():
             acopy(slot, slot).wait_recv()
-            total = acc[r, slot] + own[r]
-            rows = pl.ds(pl.multiple_of(r * t, t), t)
-            y_ref[rows, :] = total[0:t].astype(BF16)
-            dx_ref[rows, :] = total[t:2 * t].astype(BF16)
-            dg_ref[r] = total[2 * t:2 * t + top]
+            own[r] += acc[r, slot]
+            out[r] = own[r, 0:2 * t, :].astype(BF16)
+            for cp in results(r):
+                cp.start()
 
         return carry
 
     lax.fori_loop(0, (n + LAG + 1) * RINGS, step, 0)
+
+    for cp in weight_grads():
+        cp.wait()
+
+    def end(r, carry):
+        for cp in results(r):
+            cp.wait()
+        return carry
+
+    lax.fori_loop(0, RINGS, end, 0)
+
+
+def results_kernel(y_in, dx_in, dg_in, gw13_in, gw2_in, y_out, dx_out, dg_out, gw1_out, gw3_out, gw2_out,
+                   y, dx, dg, gw13, gw2, in_sem, out_sem):
+    el, ff, _ = gw2.shape
+    bufs = (gw13, gw2, y, dx, dg)
+    into = [pltpu.make_async_copy(a, b, in_sem.at[i]) for i, (a, b) in enumerate(zip((gw13_in, gw2_in, y_in, dx_in, dg_in), bufs))]
+    for cp in into:
+        cp.start()
+    t = dg.shape[2]
+    outs = []
+
+    def put(src, dst):
+        cp = pltpu.make_async_copy(src, dst, out_sem.at[len(outs)])
+        cp.start()
+        outs.append(cp)
+
+    into[0].wait()
+    for e in range(el):
+        put(gw13.at[:, pl.ds(2 * e * ff, ff)], gw1_out.at[e])
+        put(gw13.at[:, pl.ds((2 * e + 1) * ff, ff)], gw3_out.at[e])
+    for cp, buf, dst in zip(into[1:4], bufs[1:4], (gw2_out, y_out, dx_out)):
+        cp.wait()
+        put(buf, dst)
+    into[4].wait()
+    for r in range(RINGS):
+        put(dg.at[r], dg_out.at[:, pl.ds(r * t, t)])
+    for cp in outs:
+        cp.wait()
 
 
 def solution(mesh):
@@ -297,29 +354,29 @@
         el, ff, _ = w2.shape
         t = tok // RINGS
         rows = 2 * t + top
-        vmem = pl.BlockSpec(memory_space=pltpu.VMEM)
         hbm = pl.BlockSpec(memory_space=pltpu.HBM)
-        dma = pltpu.SemaphoreType.DMA((RINGS, SLOTS + 1))
+        dma = pltpu.SemaphoreType.DMA((RINGS, SLOTS + 2))
         flops = 2 * n * tok * el * 9 * d * ff
-        y, dx, dg, gw1, gw3, gw2 = pl.pallas_call(
+        outs = pl.pallas_call(
             functools.partial(kernel, n, k),
             out_shape=(
                 jax.ShapeDtypeStruct((tok, d), BF16),
                 jax.ShapeDtypeStruct((tok, d), BF16),
                 jax.ShapeDtypeStruct((RINGS, top, t), F32),
-                jax.ShapeDtypeStruct((el, d, ff), F32),
-                jax.ShapeDtypeStruct((el, d, ff), F32),
+                jax.ShapeDtypeStruct((d, 2 * el * ff), F32),
                 jax.ShapeDtypeStruct((el, ff, d), F32),
             ),
             in_specs=[hbm] * 7,
-            out_specs=tuple([vmem] * 6),
+            out_specs=tuple([hbm] * 5),
             scratch_shapes=[
-                pltpu.VMEM((RINGS, SLOTS + 1, rows, d), BF16),
-                pltpu.VMEM((RINGS, SLOTS + 1, top, t), F32),
+                pltpu.VMEM((RINGS, SLOTS + 2, rows, d), BF16),
+                pltpu.VMEM((RINGS, SLOTS + 2, top, t), F32),
                 pltpu.VMEM((RINGS, SLOTS + 1, rows, d), F32),
                 pltpu.VMEM((RINGS, rows, d), F32),
                 pltpu.VMEM((rows, d), F32),
                 pltpu.VMEM((d, 2 * el * ff), F32),
+                pltpu.VMEM((el, ff, d), F32),
+                pltpu.VMEM((RINGS, 2 * t, d), BF16),
                 pltpu.VMEM((top, tok), jnp.int32),
                 pltpu.VMEM((d, el * ff), BF16),
                 pltpu.VMEM((d, el * ff), BF16),
@@ -327,6 +384,7 @@
                 pltpu.VMEM((el, d, ff), BF16),
                 pltpu.VMEM((el, 2 * ff, d), BF16),
                 pltpu.SemaphoreType.DMA((RINGS + 3, max(3, el))),
+                pltpu.SemaphoreType.DMA((RINGS + 1, 3)),
                 dma, dma, dma, dma, dma, dma,
                 pltpu.SemaphoreType.REGULAR((RINGS,)),
                 pltpu.SemaphoreType.REGULAR((RINGS,)),
@@ -336,6 +394,25 @@
             cost_estimate=pl.CostEstimate(flops=flops, bytes_accessed=4 * tok * d * 2, transcendentals=n * tok * el * ff),
             name='moe_ring',
         )(x, dy, gates.T, ridx.T, w1, w3, w2)
-        return y, dx, dg.transpose(0, 2, 1).reshape(tok, top), gw1, gw3, gw2
+        y, dx, dg, gw1, gw3, gw2 = pl.pallas_call(
+            results_kernel,
+            out_shape=(
+                jax.ShapeDtypeStruct((tok, d), BF16),
+                jax.ShapeDtypeStruct((tok, d), BF16),
+                jax.ShapeDtypeStruct((top, tok), F32),
+                jax.ShapeDtypeStruct((el, d, ff), F32),
+                jax.ShapeDtypeStruct((el, d, ff), F32),
+                jax.ShapeDtypeStruct((el, ff, d), F32),
+            ),
+            in_specs=[hbm] * 5,
+            out_specs=tuple([hbm] * 6),
+            scratch_shapes=[pltpu.VMEM(o.shape, o.dtype) for o in outs] + [
+                pltpu.SemaphoreType.DMA((5,)),
+                pltpu.SemaphoreType.DMA((2 * el + 3 + RINGS,)),
+            ],
+            compiler_params=pltpu.CompilerParams(vmem_limit_bytes=56 * 1024 * 1024),
+            name='moe_results',
+        )(*outs)
+        return y, dx, dg.T, gw1, gw3, gw2
 
     return jax.shard_map(local, mesh=mesh, in_specs=(tspec, tspec, tspec, wspec, wspec, wspec, tspec), out_specs=(tspec, tspec, tspec, gspec, gspec, gspec), check_vma=False)

time: 284 us -> 278 us (0.979)
  local copies, waits for them, and re-layouts: 6.13 us -> 0 us
    unnamed x16 -> x0, local copies, waits for them, and re-layouts: 6.13 us -> none
where the time goes in v4:
time: 278 us
  Pallas kernels  278 us (100%)
    pallas_call x1, Pallas kernels, local(): pl.pallas_call(functools.partial(kernel, n, k), out_shape=(jax.ShapeDtype...  275 us

profile of v4, /device:TPU:97, one launch (start us, length us, event | category | flops | bytes accessed | tf_op | source)
XLA Modules:
  0.0 278.2 jit_solution(12104239853219101714)
XLA Ops:
  0.6 275.1 %moe_ring.1 = (bf16[1024,256]{1,0:T(8,128)(2,1)}, bf16[1024,256]{1,0:T(8,128)(2,1)}, f32[4,8,256]{2,1,0:T(8,128)}, f32[256,512]{1,0:T(8,128)}, f32[2,128,256]{2,1,0:T(8,128)}) custom-call(bf16[1024,256]{1,0:T(8,128)(2,1)} %x_hbm.1, bf16[1024,256]{1,0:T(8,128)(2,1)} %dy_hbm.1, f32[8,1024]{1,0:T(8,128)} %bitcast.3, s32[8,1024]{1,0:T(8,128)} %bitcast.4, ...), custom_call_target="tpu_custom_call" | custom-call | flops 38654705664 | bytes 2097152 | tf_op jit(solution)/shard_map/moe_ring/pallas_call | solution.py:360
  275.8 2.4 moe_results.1

commit v5 on v4

--- a/solution.py
+++ b/solution.py
@@ -51,9 +51,9 @@
 
 
 def kernel(n, k, x_hbm, dy_hbm, g_hbm, id_hbm, w1_hbm, w3_hbm, w2_hbm,
-           y_hbm, dx_hbm, dg_hbm, gw13_hbm, gw2_hbm,
-           xs, gs, acc, own, part, gw13, gw2_ref, out, ids, w1_ref, w3_ref, w2_ref, w2t_ref, w13t_ref,
-           load_sem, out_sem, xsend, xrecv, gsend, grecv, asend, arecv, xfree, afree):
+           y_ref, dx_ref, dg_ref, gw13, gw2_ref,
+           xs, gs, acc, own, part, ids, w1_ref, w3_ref, w2_ref, w2t_ref, w13t_ref,
+           load_sem, xsend, xrecv, gsend, grecv, asend, arecv, xfree, afree):
     t = gs.shape[3]
     d = x_hbm.shape[1]
     el, ff, _ = w2_hbm.shape
@@ -61,6 +61,10 @@
     h1, h2 = neighbours(k)
     core = lax.axis_index('col') % 2
     first_expert = (lax.axis_index('row') * lax.axis_size('col') + lax.axis_index('col')) * el
+
+    barrier = pltpu.get_barrier_semaphore()
+    for dev in (*h1, *h2):
+        pl.semaphore_signal(barrier, inc=1, device_id=dev, device_id_type=MESH)
 
     def load(src, dst, i, j):
         cp = pltpu.make_async_copy(src, dst, load_sem.at[i, j])
@@ -78,10 +82,6 @@
         cols = pl.ds(e * ff, ff)
         later.append(load(w1_hbm.at[e], w1_ref.at[:, cols], RINGS + 1, e))
         later.append(load(w3_hbm.at[e], w3_ref.at[:, cols], RINGS + 2, e))
-
-    barrier = pltpu.get_barrier_semaphore()
-    for dev in (*h1, *h2):
-        pl.semaphore_signal(barrier, inc=1, device_id=dev, device_id_type=MESH)
 
     for cp in first:
         cp.wait()
@@ -180,16 +180,6 @@
         w13t_ref[e, 0:ff, :] = w1_ref[:, cols].astype(F32).T.astype(BF16)
         w13t_ref[e, ff:2 * ff, :] = w3_ref[:, cols].astype(F32).T.astype(BF16)
 
-    def weight_grads():
-        return (pltpu.make_async_copy(gw13, gw13_hbm, out_sem.at[RINGS, 0]),
-                pltpu.make_async_copy(gw2_ref, gw2_hbm, out_sem.at[RINGS, 1]))
-
-    def results(r):
-        rows = pl.ds(pl.multiple_of(r * t, t), t)
-        return (pltpu.make_async_copy(out.at[r, pl.ds(0, t)], y_hbm.at[rows], out_sem.at[r, 0]),
-                pltpu.make_async_copy(out.at[r, pl.ds(t, t)], dx_hbm.at[rows], out_sem.at[r, 1]),
-                pltpu.make_async_copy(own.at[r, pl.ds(2 * t, top)], dg_hbm.at[r], out_sem.at[r, 2]))
-
     def step(i, carry):
         link, r, nxt, prv = ring(i % RINGS)
         st = i // RINGS - 1 + link
@@ -278,11 +268,6 @@
             tile(r, HOME)
             own[r] = part[...]
 
-        @pl.when(i == n * RINGS + 2)
-        def _():
-            for cp in weight_grads():
-                cp.start()
-
         @pl.when((st == n - 1) & (link == 0))
         def _():
             acopy(SLOTS, SLOTS).wait_recv()
@@ -291,52 +276,30 @@
         @pl.when(st == n)
         def _():
             acopy(slot, slot).wait_recv()
-            own[r] += acc[r, slot]
-            out[r] = own[r, 0:2 * t, :].astype(BF16)
-            for cp in results(r):
-                cp.start()
+            total = acc[r, slot] + own[r]
+            rows = pl.ds(pl.multiple_of(r * t, t), t)
+            y_ref[rows, :] = total[0:t].astype(BF16)
+            dx_ref[rows, :] = total[t:2 * t].astype(BF16)
+            dg_ref[r] = total[2 * t:2 * t + top]
 
         return carry
 
     lax.fori_loop(0, (n + LAG + 1) * RINGS, step, 0)
 
-    for cp in weight_grads():
-        cp.wait()
-
-    def end(r, carry):
-        for cp in results(r):
-            cp.wait()
-        return carry
-
-    lax.fori_loop(0, RINGS, end, 0)
-
-
-def results_kernel(y_in, dx_in, dg_in, gw13_in, gw2_in, y_out, dx_out, dg_out, gw1_out, gw3_out, gw2_out,
-                   y, dx, dg, gw13, gw2, in_sem, out_sem):
+
+def results_kernel(y, dx, dg, gw13, gw2, y_out, dx_out, dg_out, gw1_out, gw3_out, gw2_out, sem):
     el, ff, _ = gw2.shape
-    bufs = (gw13, gw2, y, dx, dg)
-    into = [pltpu.make_async_copy(a, b, in_sem.at[i]) for i, (a, b) in enumerate(zip((gw13_in, gw2_in, y_in, dx_in, dg_in), bufs))]
-    for cp in into:
+    t = dg.shape[2]
+    pairs = [(y, y_out), (dx, dx_out), (gw2, gw2_out)]
+    for e in range(el):
+        pairs.append((gw13.at[:, pl.ds(2 * e * ff, ff)], gw1_out.at[e]))
+        pairs.append((gw13.at[:, pl.ds((2 * e + 1) * ff, ff)], gw3_out.at[e]))
+    for r in range(RINGS):
+        pairs.append((dg.at[r], dg_out.at[:, pl.ds(r * t, t)]))
+    copies = [pltpu.make_async_copy(a, b, sem.at[i]) for i, (a, b) in enumerate(pairs)]
+    for cp in copies:
         cp.start()
-    t = dg.shape[2]
-    outs = []
-
-    def put(src, dst):
-        cp = pltpu.make_async_copy(src, dst, out_sem.at[len(outs)])
-        cp.start()
-        outs.append(cp)
-
-    into[0].wait()
-    for e in range(el):
-        put(gw13.at[:, pl.ds(2 * e * ff, ff)], gw1_out.at[e])
-        put(gw13.at[:, pl.ds((2 * e + 1) * ff, ff)], gw3_out.at[e])
-    for cp, buf, dst in zip(into[1:4], bufs[1:4], (gw2_out, y_out, dx_out)):
-        cp.wait()
-        put(buf, dst)
-    into[4].wait()
-    for r in range(RINGS):
-        put(dg.at[r], dg_out.at[:, pl.ds(r * t, t)])
-    for cp in outs:
+    for cp in copies:
         cp.wait()
 
 
@@ -354,29 +317,27 @@
         el, ff, _ = w2.shape
         t = tok // RINGS
         rows = 2 * t + top
+        vmem = pl.BlockSpec(memory_space=pltpu.VMEM)
         hbm = pl.BlockSpec(memory_space=pltpu.HBM)
         dma = pltpu.SemaphoreType.DMA((RINGS, SLOTS + 2))
         flops = 2 * n * tok * el * 9 * d * ff
         outs = pl.pallas_call(
             functools.partial(kernel, n, k),
             out_shape=(
-                jax.ShapeDtypeStruct((tok, d), BF16),
-                jax.ShapeDtypeStruct((tok, d), BF16),
-                jax.ShapeDtypeStruct((RINGS, top, t), F32),
-                jax.ShapeDtypeStruct((d, 2 * el * ff), F32),
-                jax.ShapeDtypeStruct((el, ff, d), F32),
+                pltpu.VMEM((tok, d), BF16),
+                pltpu.VMEM((tok, d), BF16),
+                pltpu.VMEM((RINGS, top, t), F32),
+                pltpu.VMEM((d, 2 * el * ff), F32),
+                pltpu.VMEM((el, ff, d), F32),
             ),
             in_specs=[hbm] * 7,
-            out_specs=tuple([hbm] * 5),
+            out_specs=tuple([vmem] * 5),
             scratch_shapes=[
                 pltpu.VMEM((RINGS, SLOTS + 2, rows, d), BF16),
                 pltpu.VMEM((RINGS, SLOTS + 2, top, t), F32),
                 pltpu.VMEM((RINGS, SLOTS + 1, rows, d), F32),
                 pltpu.VMEM((RINGS, rows, d), F32),
                 pltpu.VMEM((rows, d), F32),
-                pltpu.VMEM((d, 2 * el * ff), F32),
-                pltpu.VMEM((el, ff, d), F32),
-                pltpu.VMEM((RINGS, 2 * t, d), BF16),
                 pltpu.VMEM((top, tok), jnp.int32),
                 pltpu.VMEM((d, el * ff), BF16),
                 pltpu.VMEM((d, el * ff), BF16),
@@ -384,16 +345,15 @@
                 pltpu.VMEM((el, d, ff), BF16),
                 pltpu.VMEM((el, 2 * ff, d), BF16),
                 pltpu.SemaphoreType.DMA((RINGS + 3, max(3, el))),
-                pltpu.SemaphoreType.DMA((RINGS + 1, 3)),
                 dma, dma, dma, dma, dma, dma,
                 pltpu.SemaphoreType.REGULAR((RINGS,)),
                 pltpu.SemaphoreType.REGULAR((RINGS,)),
             ],
             compiler_params=pltpu.CompilerParams(
-                collective_id=0, has_side_effects=True, vmem_limit_bytes=56 * 1024 * 1024),
+                collective_id=0, has_side_effects=True, vmem_limit_bytes=48 * 1024 * 1024),
             cost_estimate=pl.CostEstimate(flops=flops, bytes_accessed=4 * tok * d * 2, transcendentals=n * tok * el * ff),
             name='moe_ring',
-        )(x, dy, gates.T, ridx.T, w1, w3, w2)
+        )(*(pltpu.with_memory_space_constraint(a, pltpu.HBM) for a in (x, dy, gates.T, ridx.T, w1, w3, w2)))
         y, dx, dg, gw1, gw3, gw2 = pl.pallas_call(
             results_kernel,
             out_shape=(
@@ -404,15 +364,12 @@
                 jax.ShapeDtypeStruct((el, d, ff), F32),
                 jax.ShapeDtypeStruct((el, ff, d), F32),
             ),
-            in_specs=[hbm] * 5,
+            in_specs=[vmem] * 5,
             out_specs=tuple([hbm] * 6),
-            scratch_shapes=[pltpu.VMEM(o.shape, o.dtype) for o in outs] + [
-                pltpu.SemaphoreType.DMA((5,)),
-                pltpu.SemaphoreType.DMA((2 * el + 3 + RINGS,)),
-            ],
-            compiler_params=pltpu.CompilerParams(vmem_limit_bytes=56 * 1024 * 1024),
+            scratch_shapes=[pltpu.SemaphoreType.DMA((2 * el + 3 + RINGS,))],
+            compiler_params=pltpu.CompilerParams(vmem_limit_bytes=48 * 1024 * 1024),
             name='moe_results',
-        )(*outs)
+        )(*(pltpu.with_memory_space_constraint(a, pltpu.VMEM) for a in outs))
         return y, dx, dg.T, gw1, gw3, gw2
 
     return jax.shard_map(local, mesh=mesh, in_specs=(tspec, tspec, tspec, wspec, wspec, wspec, tspec), out_specs=(tspec, tspec, tspec, gspec, gspec, gspec), check_vma=False)

time: 278 us -> 277 us (level)
  no operation moved by 1% of the time
where the time goes in v5:
time: 277 us
  Pallas kernels  276 us (100%)
    pallas_call x1, Pallas kernels, local(): pl.pallas_call(functools.partial(kernel, n, k), out_shape=(pltpu.VMEM((to...  275 us

profile of v5, /device:TPU:97, one launch (start us, length us, event | category | flops | bytes accessed | tf_op | source)
XLA Modules:
  0.0 276.8 jit_solution(5439063129096399276)
XLA Ops:
  0.6 274.8 %moe_ring.1 = (bf16[1024,256]{1,0:T(8,128)(2,1)S(1)}, bf16[1024,256]{1,0:T(8,128)(2,1)S(1)}, f32[4,8,256]{2,1,0:T(8,128)S(1)}, f32[256,512]{1,0:T(8,128)S(1)}, f32[2,128,256]{2,1,0:T(8,128)S(1)}) custom-call(bf16[1024,256]{1,0:T(8,128)(2,1)} %x_hbm.1, bf16[1024,256]{1,0:T(8,128)(2,1)} %dy_hbm.1, f32[8,1024]{1,0:T(8,128)} %bitcast.3, s32[8,1024]{1,0:T(8,128)} %bitcast.4, ...), custom_call_target="tpu_custom_call" | custom-call | flops 38654705664 | bytes 2097152 | tf_op jit(solution)/shard_map/moe_ring/pallas_call | solution.py:324
  275.4 1.3 moe_results.1

commit v6 on v5

--- a/solution.py
+++ b/solution.py
@@ -91,10 +91,10 @@
     gw2_ref[...] = jnp.zeros_like(gw2_ref)
     pl.semaphore_wait(barrier, 4)
 
-    def tile(r, slot):
+    def tile(r, slot, gslot):
         x = xs[r, slot, 0:t, :]
         dy = xs[r, slot, t:2 * t, :]
-        gates = gs[r, slot, 0:top, :]
+        gates = gs[r, gslot]
         dest = xs[r, slot, 2 * t:2 * t + top, :].astype(F32)
         hit = [dest == (first_expert + e).astype(F32) for e in range(el)]
         sub = lax.broadcasted_iota(jnp.int32, gates.shape, 0)
@@ -137,10 +137,9 @@
         part[0:t, :] = y
         part[t:2 * t, :] = dx
         dgr = dgc.T
-        dg = jnp.zeros_like(gates)
         for e in range(el):
-            dg = jnp.where(hit[e], dgr[e:e + 1, :], dg)
-        part[2 * t:2 * t + top, :] = dg
+            gates = jnp.where(hit[e], dgr[e:e + 1, :], gates)
+        gs[r, gslot] = gates
 
     def ring(i):
         link = i // 2
@@ -155,18 +154,17 @@
             src_ref=buf.at[r, a], dst_ref=buf.at[r, b], send_sem=sends.at[r, a if s is None else s],
             recv_sem=recvs.at[r, b], device_id=dev, device_id_type=MESH)
 
-    def xcopies(r, a, b, dev, s=None):
-        return send(gs, gsend, grecv, r, a, b, dev, s), send(xs, xsend, xrecv, r, a, b, dev, s)
+    def xcopy(r, a, b, dev, s=None):
+        return send(xs, xsend, xrecv, r, a, b, dev, s)
 
     def begin(i, carry):
         link, r, nxt, prv = ring(RINGS - 1 - i)
-        for cp in xcopies(r, HOME, 1, nxt):
-            cp.start()
+        send(gs, gsend, grecv, r, HOME, 1, nxt).start()
+        xcopy(r, HOME, 1, nxt).start()
 
         @pl.when(link == 1)
         def _():
-            for cp in xcopies(r, HOME, SLOTS, prv, SLOTS):
-                cp.start()
+            xcopy(r, HOME, SLOTS, prv, SLOTS).start()
 
         return carry
 
@@ -195,20 +193,21 @@
         def acopy(a, b):
             return send(acc, asend, arecv, r, a, b, nxt)
 
+        def gcopy(a, b):
+            return send(gs, gsend, grecv, r, a, b, nxt)
+
         @pl.when((st >= 2) & (st <= n - 1 - link))
         def _():
-            for cp in xcopies(r, gone, gone, nxt):
-                cp.wait_send()
+            xcopy(r, gone, gone, nxt).wait_send()
 
         @pl.when(st == 2)
         def _():
-            for cp in xcopies(r, HOME, HOME, nxt):
-                cp.wait_send()
+            gcopy(HOME, HOME).wait_send()
+            xcopy(r, HOME, HOME, nxt).wait_send()
 
         @pl.when((st == 2) & (link == 1))
         def _():
-            for cp in xcopies(r, HOME, SLOTS, prv, SLOTS):
-                cp.wait_send()
+            xcopy(r, HOME, SLOTS, prv, SLOTS).wait_send()
 
         @pl.when((st >= 2) & (st <= n - 1 - SLOTS + link))
         def _():
@@ -216,6 +215,7 @@
 
         @pl.when((done >= 1) & (done <= n - 1))
         def _():
+            gcopy(dslot, dslot).wait_send()
             acopy(dslot, dslot).wait_send()
 
         @pl.when((done >= 1) & (done <= n - SLOTS))
@@ -224,14 +224,9 @@
 
         @pl.when((st >= 0) & (st <= n - 1))
         def _():
-            @pl.when(st >= 1)
-            def _():
-                tile(r, xslot)
-
             @pl.when(st <= n - 2)
             def _():
-                for cp in xcopies(r, into_x, into_x, nxt):
-                    cp.wait_recv()
+                xcopy(r, into_x, into_x, nxt).wait_recv()
 
             @pl.when(st <= n - 3 - link)
             def _():
@@ -239,33 +234,39 @@
                 def _():
                     pl.semaphore_wait(xfree.at[r], 1)
 
-                for cp in xcopies(r, into, two, nxt):
-                    cp.start()
-
-            @pl.when((st >= 1) & (st <= 2 - link))
-            def _():
-                acc[r, slot] = part[...]
-
-            @pl.when(st >= 3 - link)
-            def _():
-                acopy(slot, slot).wait_recv()
-                acc[r, slot] += part[...]
-
-            @pl.when((st == 1) & (link == 1))
-            def _():
-                send(acc, asend, arecv, r, 1, SLOTS, prv).start()
-
-            @pl.when(st >= 1 + link)
-            def _():
+                xcopy(r, into, two, nxt).start()
+
+            @pl.when(st >= 1)
+            def _():
+                gcopy(slot, slot).wait_recv()
+                tile(r, xslot, slot)
+
                 @pl.when(st >= SLOTS)
                 def _():
                     pl.semaphore_wait(afree.at[r], 1)
 
+                gcopy(slot, into).start()
+
+            @pl.when((st >= 1) & (st <= 2 - link))
+            def _():
+                acc[r, slot] = part[...]
+
+            @pl.when(st >= 3 - link)
+            def _():
+                acopy(slot, slot).wait_recv()
+                acc[r, slot] += part[...]
+
+            @pl.when((st == 1) & (link == 1))
+            def _():
+                send(acc, asend, arecv, r, 1, SLOTS, prv).start()
+
+            @pl.when(st >= 1 + link)
+            def _():
                 acopy(slot, into).start()
 
         @pl.when(st == OWN_STEP)
         def _():
-            tile(r, HOME)
+            tile(r, HOME, HOME)
             own[r] = part[...]
 
         @pl.when((st == n - 1) & (link == 0))
@@ -275,12 +276,14 @@
 
         @pl.when(st == n)
         def _():
+            gcopy(slot, slot).wait_recv()
             acopy(slot, slot).wait_recv()
             total = acc[r, slot] + own[r]
             rows = pl.ds(pl.multiple_of(r * t, t), t)
             y_ref[rows, :] = total[0:t].astype(BF16)
             dx_ref[rows, :] = total[t:2 * t].astype(BF16)
-            dg_ref[r] = total[2 * t:2 * t + top]
+            mine = xs[r, HOME, 2 * t:2 * t + top, :].astype(F32) - first_expert.astype(F32)
+            dg_ref[r] = jnp.where((mine >= 0.0) & (mine < el), gs[r, HOME], gs[r, slot])
 
         return carry
 
@@ -335,9 +338,9 @@
             scratch_shapes=[
                 pltpu.VMEM((RINGS, SLOTS + 2, rows, d), BF16),
                 pltpu.VMEM((RINGS, SLOTS + 2, top, t), F32),
-                pltpu.VMEM((RINGS, SLOTS + 1, rows, d), F32),
-                pltpu.VMEM((RINGS, rows, d), F32),
-                pltpu.VMEM((rows, d), F32),
+                pltpu.VMEM((RINGS, SLOTS + 1, 2 * t, d), F32),
+                pltpu.VMEM((RINGS, 2 * t, d), F32),
+                pltpu.VMEM((2 * t, d), F32),
                 pltpu.VMEM((top, tok), jnp.int32),
                 pltpu.VMEM((d, el * ff), BF16),
                 pltpu.VMEM((d, el * ff), BF16),

time: 277 us -> 274 us (0.989)
  no operation moved by 1% of the time
where the time goes in v6:
time: 274 us
  Pallas kernels  274 us (100%)
    pallas_call x1, Pallas kernels, local(): pl.pallas_call(functools.partial(kernel, n, k), out_shape=(pltpu.VMEM((to...  272 us

profile of v6, /device:TPU:97, one launch (start us, length us, event | category | flops | bytes accessed | tf_op | source)
XLA Modules:
  0.0 274.2 jit_solution(12869118540347834460)
XLA Ops:
  0.6 272.2 %moe_ring.1 = (bf16[1024,256]{1,0:T(8,128)(2,1)S(1)}, bf16[1024,256]{1,0:T(8,128)(2,1)S(1)}, f32[4,8,256]{2,1,0:T(8,128)S(1)}, f32[256,512]{1,0:T(8,128)S(1)}, f32[2,128,256]{2,1,0:T(8,128)S(1)}) custom-call(bf16[1024,256]{1,0:T(8,128)(2,1)} %x_hbm.1, bf16[1024,256]{1,0:T(8,128)(2,1)} %dy_hbm.1, f32[8,1024]{1,0:T(8,128)} %bitcast.3, s32[8,1024]{1,0:T(8,128)} %bitcast.4, ...), custom_call_target="tpu_custom_call" | custom-call | flops 38654705664 | bytes 2097152 | tf_op jit(solution)/shard_map/moe_ring/pallas_call | solution.py:327
  272.9 1.3 moe_results.1

commit v7 on v6

--- a/solution.py
+++ b/solution.py
@@ -142,8 +142,8 @@
         gs[r, gslot] = gates
 
     def ring(i):
-        link = i // 2
-        cyc = i % 2
+        link = i % 2
+        cyc = i // 2
         back = core + link * (1 - 2 * core)
         fwd = pick(cyc, h1[0], h2[0])
         bwd = pick(cyc, h1[1], h2[1])

time: 274 us -> 277 us (1.011)
  Pallas kernels: 274 us -> 277 us
    pallas_call x1, Pallas kernels: 272 us -> 275 us  [local(): pl.pallas_call(functools.partial(kernel, n, k), out_shape=(pltpu.VMEM((to...]
where the time goes in v7:
time: 277 us
  Pallas kernels  277 us (100%)
    pallas_call x1, Pallas kernels, local(): pl.pallas_call(functools.partial(kernel, n, k), out_shape=(pltpu.VMEM((to...  275 us

profile of v7, /device:TPU:97, one launch (start us, length us, event | category | flops | bytes accessed | tf_op | source)
XLA Modules:
  0.0 277.3 jit_solution(12675243686342865404)
XLA Ops:
  0.6 275.3 %moe_ring.1 = (bf16[1024,256]{1,0:T(8,128)(2,1)S(1)}, bf16[1024,256]{1,0:T(8,128)(2,1)S(1)}, f32[4,8,256]{2,1,0:T(8,128)S(1)}, f32[256,512]{1,0:T(8,128)S(1)}, f32[2,128,256]{2,1,0:T(8,128)S(1)}) custom-call(bf16[1024,256]{1,0:T(8,128)(2,1)} %x_hbm.1, bf16[1024,256]{1,0:T(8,128)(2,1)} %dy_hbm.1, f32[8,1024]{1,0:T(8,128)} %bitcast.3, s32[8,1024]{1,0:T(8,128)} %bitcast.4, ...), custom_call_target="tpu_custom_call" | custom-call | flops 38654705664 | bytes 2097152 | tf_op jit(solution)/shard_map/moe_ring/pallas_call | solution.py:327
  275.9 1.3 moe_results.1
